TPU v7x, 32 devices: a 4x2x2 block of a 4x4x8 slice. The times are simulated.
32 devices in a mesh: dp: 4 (over y, z), tp: 8 (over x, core).
Axes of the slice: x: 4, y: 2, z: 2, core: 2. Of those that a mesh axis runs over, the one named last changes fastest.
The devices are a block of a 4x4x8 slice.
Arguments:
- hidden: bfloat16 [4, 768, 2560], P('dp'), parts along dimension 0
- norm_w: bfloat16 [2, 2560], replicated
- w_z: bfloat16 [2, 2560, 5120], P(None, None, 'tp')
- w_x: bfloat16 [2, 2560, 5120], P(None, None, 'tp')
- w_bc: bfloat16 [2, 2560, 256], replicated
- w_dt: bfloat16 [2, 2560, 80], P(None, None, 'tp')
- conv_x: bfloat16 [2, 4, 5120], P(None, None, 'tp')
- conv_bc: bfloat16 [2, 4, 256], replicated
- bias_x: bfloat16 [2, 5120], P(None, 'tp')
- bias_bc: bfloat16 [2, 256], replicated
- dt_bias: float32 [2, 80], P(None, 'tp')
- a_log: float32 [2, 80], P(None, 'tp')
- d_skip: float32 [2, 80], P(None, 'tp')
- gate_w: bfloat16 [2, 5120], P(None, 'tp')
- w_out: bfloat16 [2, 5120, 2560], P(None, 'tp')
Outputs:
- output: bfloat16 [4, 768, 2560], P('dp'), parts along dimension 0
There are 4 independent parts. A program takes and returns all parts, laid end to end along the dimension named above; an argument that names none is the same for every part.
All inputs are finite; a program needn't handle non-finite values.
Results may differ from a plain program's by a relative error of at most 0.014167.
Values sent between devices are 32-bit elements.
A program may use at most 768 MiB of HBM per device.

v0:
```python
import jax
import jax.numpy as jnp
from jax import lax
from jax.sharding import PartitionSpec as P

EPSILON = 1e-5
CONV_WIDTH = 4
BLOCK_LEN = 256
FULL_PRECISION = lax.Precision.HIGHEST


def causal_conv(seq_in, kernel, conv_bias):
    n_steps = seq_in.shape[1]
    padded = jnp.pad(seq_in, ((0, 0), (CONV_WIDTH - 1, 0), (0, 0)))
    conv_sum = conv_bias.astype(jnp.float32)
    for tap_index in range(CONV_WIDTH):
        conv_sum = conv_sum + padded[:, tap_index:tap_index + n_steps, :].astype(jnp.float32) * kernel[tap_index].astype(jnp.float32)
    return conv_sum


def ssd_blocks(x_heads, dt_val, a_vals, b_in, c_in):
    n_batch, n_steps, n_heads, head_width = x_heads.shape
    n_state = b_in.shape[-1]
    n_blocks = n_steps // BLOCK_LEN
    x_blocks = x_heads.reshape(n_batch, n_blocks, BLOCK_LEN, n_heads, head_width)
    dt_blocks = dt_val.reshape(n_batch, n_blocks, BLOCK_LEN, n_heads)
    b_blocks = b_in.reshape(n_batch, n_blocks, BLOCK_LEN, n_state)
    c_blocks = c_in.reshape(n_batch, n_blocks, BLOCK_LEN, n_state)
    a_cum = jnp.cumsum(a_vals.reshape(n_batch, n_blocks, BLOCK_LEN, n_heads), axis=2)
    a_cum_t = jnp.swapaxes(a_cum, 2, 3)
    seg_sum = a_cum_t[..., :, None] - a_cum_t[..., None, :]
    step_ids = jnp.arange(BLOCK_LEN)
    lower_tri = step_ids[:, None] >= step_ids[None, :]
    c_dot_b = jnp.einsum('bcin,bcjn->bcij', c_blocks, b_blocks, precision=FULL_PRECISION)
    mix_mat = jnp.where(lower_tri, jnp.exp(jnp.minimum(seg_sum, 0.0)), 0.0) * c_dot_b[:, :, None]
    x_dt = x_blocks * dt_blocks[..., None]
    y_in = jnp.einsum('bchij,bcjhp->bcihp', mix_mat, x_dt, precision=FULL_PRECISION)
    a_last = a_cum[:, :, -1, :]
    tail_decay = jnp.exp(a_last[:, :, None, :] - a_cum)
    block_states = jnp.einsum('bcjn,bcjhp->bchpn', b_blocks, x_dt * tail_decay[..., None], precision=FULL_PRECISION)
    block_ends = jnp.swapaxes(jnp.cumsum(a_last, axis=1), 1, 2)
    block_starts = block_ends - jnp.swapaxes(a_last, 1, 2)
    block_ids = jnp.arange(n_blocks)
    earlier = block_ids[:, None] > block_ids[None, :]
    carry_mat = jnp.where(earlier, jnp.exp(jnp.minimum(block_starts[..., :, None] - block_ends[..., None, :], 0.0)), 0.0)
    s_in = jnp.einsum('bhck,bkhpn->bchpn', carry_mat, block_states, precision=FULL_PRECISION)
    y_st = jnp.einsum('bcin,bchpn->bcihp', c_blocks, s_in, precision=FULL_PRECISION) * jnp.exp(a_cum)[..., None]
    return (y_in + y_st).reshape(n_batch, n_steps, n_heads, head_width)


def mixer_layer(current, norm_w, w_z, w_x, w_bc, w_dt, conv_x, conv_bc, bias_x, bias_bc, dt_bias, a_log, d_skip, gate_w, w_out, inner_width):
    n_batch = current.shape[0]
    n_steps = current.shape[1]
    n_heads = dt_bias.shape[0]
    local_width = w_x.shape[-1]
    state_dim = w_bc.shape[-1] // 2
    residual = current.astype(jnp.float32)
    normed = (residual * lax.rsqrt(jnp.mean(residual * residual, axis=-1, keepdims=True) + EPSILON) * norm_w.astype(jnp.float32)).astype(jnp.bfloat16)
    gate_z = jnp.einsum('btd,de->bte', normed, w_z, preferred_element_type=jnp.float32).astype(jnp.bfloat16)
    x_pre = jnp.einsum('btd,de->bte', normed, w_x, preferred_element_type=jnp.float32).astype(jnp.bfloat16)
    bc_pre = jnp.einsum('btd,de->bte', normed, w_bc, preferred_element_type=jnp.float32).astype(jnp.bfloat16)
    dt_pre = jnp.einsum('btd,de->bte', normed, w_dt, preferred_element_type=jnp.float32).astype(jnp.bfloat16)
    x_act = jax.nn.silu(causal_conv(x_pre, conv_x, bias_x))
    bc_act = jax.nn.silu(causal_conv(bc_pre, conv_bc, bias_bc))
    dt_val = jax.nn.softplus(dt_pre.astype(jnp.float32) + dt_bias)
    a_vals = -dt_val * jnp.exp(a_log)
    x_heads = x_act.reshape(n_batch, n_steps, n_heads, local_width // n_heads)
    y_heads = ssd_blocks(x_heads, dt_val, a_vals, bc_act[..., :state_dim], bc_act[..., state_dim:]) + d_skip[:, None] * x_heads
    gated_v = y_heads.reshape(n_batch, n_steps, local_width) * jax.nn.silu(gate_z.astype(jnp.float32))
    part_sq = jnp.sum(gated_v * gated_v, axis=-1, keepdims=True)
    total_sq = lax.psum(part_sq, 'tp')
    normed_y = (gated_v * lax.rsqrt(total_sq / inner_width + EPSILON) * gate_w.astype(jnp.float32)).astype(jnp.bfloat16)
    part_out = jnp.einsum('bte,ed->btd', normed_y, w_out, preferred_element_type=jnp.float32)
    full_out = lax.psum(part_out, 'tp')
    return (residual + full_out).astype(jnp.bfloat16)


def solution(mesh):
    tp_size = mesh.shape['tp']
    rep_spec = P()
    col_spec = P(None, None, 'tp')
    vec_spec = P(None, 'tp')
    in_specs = (P('dp'), rep_spec, col_spec, col_spec, rep_spec, col_spec, col_spec, rep_spec, vec_spec, rep_spec, vec_spec, vec_spec, vec_spec, vec_spec, P(None, 'tp', None))

    def device_forward(hidden, norm_w, w_z, w_x, w_bc, w_dt, conv_x, conv_bc, bias_x, bias_bc, dt_bias, a_log, d_skip, gate_w, w_out):
        inner_width = w_x.shape[-1] * tp_size
        current = hidden
        for layer_idx in range(norm_w.shape[0]):
            current = mixer_layer(current, norm_w[layer_idx], w_z[layer_idx], w_x[layer_idx], w_bc[layer_idx], w_dt[layer_idx], conv_x[layer_idx], conv_bc[layer_idx], bias_x[layer_idx], bias_bc[layer_idx], dt_bias[layer_idx], a_log[layer_idx], d_skip[layer_idx], gate_w[layer_idx], w_out[layer_idx], inner_width)
        return current

    return jax.shard_map(device_forward, mesh=mesh, in_specs=in_specs, out_specs=P('dp'), check_vma=False)
```

profile of v0, /device:TPU:81, one launch (start us, length us, event | category | flops | bytes accessed | tf_op | source)
XLA Modules:
  0.0 383.4 jit_solution(15717373884194749551)
XLA Ops:
  7.9 2.9 fusion
  11.5 0.8 fusion.139
  12.9 1.2 negate_multiply_fusion.1
  14.2 1.7 reduce-window.14
  22.4 3.9 %fusion.88 = bf16[768,256]{1,0:T(8,128)(2,1)S(1)} fusion(bf16[2,2560,256]{2,1,0:T(8,128)(2,1)} %param.19, bf16[1,768,2560]{2,1,0:T(8,128)(2,1)} %param.15, f32[2560]{0:T(1024)S(1)} %get-tuple-element.14, f32[768]{0:T(1024)S(1)} %add_rsqrt_fusion.1), kind=kOutput, calls=%fused_computation.106 | convolution fusion | flops 1014693888 | bytes 5649408 | tf_op jit(solution)/shard_map/btd,de->bte/dot_general | solution.py:61
  26.9 5.2 %fusion.64 = bf16[768,640]{1,0:T(8,128)(2,1)S(1)} fusion(bf16[2,2560,640]{2,1,0:T(8,128)(2,1)} %param.18, bf16[1,768,2560]{2,1,0:T(8,128)(2,1)S(1)} %copy-done.1, f32[2560]{0:T(1024)S(1)} %get-tuple-element.14, f32[768]{0:T(1024)S(1)} %add_rsqrt_fusion.1), kind=kOutput, calls=%fused_computation.88 | convolution fusion | flops 2524938240 | bytes 8205312 | tf_op jit(solution)/shard_map/btd,de->bte/dot_general | solution.py:60
  32.1 1.3 divide_multiply_fusion.1
  33.4 1.3 copy-done.6
  34.7 1.8 copy.78
  36.5 3.1 reshape_reshape.6
  39.6 0.8 fusion.140
  40.4 1.1 broadcast_multiply_fusion.2
  41.6 2.0 fusion.61
  43.5 2.9 convolution_bitcast_fusion.3
  46.4 9.3 %fusion.14 = f32[3,10,64,256]{3,2,1,0:T(8,128)S(1)} fusion(f32[3,256,256]{2,1,0:T(8,128)S(1)} %fusion.140, f32[3,10,256]{2,1,0:T(8,128)S(1)} %copy-done.13, pred[256,256]{1,0:T(8,128)(4,1)S(1)} %copy-done.11, f32[3,256,10,64]{1,0,3,2:T(4,128)S(1)} %get-tuple-element.28), kind=kOutput, calls=%fused_computation.20 | convolution fusion | flops 1517813760 | bytes 4814848 | tf_op jit(solution)/shard_map/bchij,bcjhp->bcihp/dot_general | solution.py:37
  55.7 1.8 bitcast_add_fusion.1
  57.6 1.4 copy.97
  58.9 1.7 copy.142
  60.7 3.0 copy.98
  63.7 8.4 %multiply_reduce_fusion.1 = (f32[768]{0:T(1024)S(1)}, f32[768,640]{1,0:T(8,128)}) fusion(bf16[2,2560,640]{2,1,0:T(8,128)(2,1)} %param.17, bf16[1,768,2560]{2,1,0:T(8,128)(2,1)} %param.15, f32[2560]{0:T(1024)S(1)} %copy-done.20, f32[768]{0:T(1024)S(1)} %copy-done.27, f32[768,640]{1,0:T(8,128)} %copy.98, f32[1,768,640]{2,1,0:T(8,128)S(1)} %copy-done.7, ...), kind=kOutput, calls=%fused_computation.86 | convolution fusion | flops 2529852672 | bytes 13126144 | tf_op jit(solution)/shard_map/btd,de->bte/dot_general | solution.py:59
  72.1 13.9 %psum.28 = f32[1,768,1]{1,2,0:T(1,128)S(1)} all-reduce(f32[1,768,1]{1,2,0:T(1,128)S(1)} %broadcast_in_dim.24), channel_id=1, replica_groups=mesh['dp'=4,'tp'=8] {'tp'}, use_global_device_ids=true, to_apply=%region_5.6 | all-reduce | flops 768 | bytes 6144 | tf_op jit(solution)/shard_map/psum | solution.py:71
  86.0 8.9 %convolution_bitcast_fusion.1 = f32[1,768,2560]{2,1,0:T(8,128)} fusion(bf16[2,640,2560]{2,1,0:T(8,128)(2,1)} %param.29, f32[768,640]{1,0:T(8,128)} %get-tuple-element.56, f32[640]{0:T(1024)S(1)} %copy-done.30, f32[768]{0:T(1024)S(1)} %rsqrt_reduce_fusion.1), kind=kOutput, calls=%fused_computation.27 | convolution fusion | flops 2518056960 | bytes 13112832 | tf_op jit(solution)/shard_map/bte,ed->btd/dot_general | solution.py:73
  95.6 0.7 mul.601
  96.3 94.1 %all-reduce.7.cloned.1.call-done = f32[1,768,2560]{2,1,0:T(8,128)} async-done(((f32[1,768,2560]{2,1,0:T(8,128)}), f32[1,768,2560]{2,1,0:T(8,128)}) %all-reduce.7.cloned.1.call-update) | async-done | bytes 7864336 | tf_op jit(solution)/shard_map/psum | solution.py:74
  190.4 5.8 %fusion.4 = (f32[768]{0:T(1024)S(1)}, bf16[1,768,2560]{2,1,0:T(8,128)(2,1)S(1)}) fusion(f32[1,768,2560]{2,1,0:T(8,128)} %all-reduce.7.cloned.1.call-done, bf16[1,768,2560]{2,1,0:T(8,128)(2,1)} %param.15), kind=kLoop, calls=%fused_computation.10 | loop fusion | flops 11795712 | bytes 15731712 | tf_op jit(solution)/shard_map/reduce_sum | solution.py:58
  196.2 1.2 negate_multiply_fusion
  198.2 1.7 reduce-window.16
  201.0 3.9 %fusion.91 = bf16[768,256]{1,0:T(8,128)(2,1)S(1)} fusion(bf16[2,2560,256]{2,1,0:T(8,128)(2,1)} %param.19, bf16[1,768,2560]{2,1,0:T(8,128)(2,1)} %copy-done.2, f32[2560]{0:T(1024)S(1)} %copy-done.17, f32[768]{0:T(1024)S(1)} %add_rsqrt_fusion), kind=kOutput, calls=%fused_computation.107 | convolution fusion | flops 1014693888 | bytes 5649408 | tf_op jit(solution)/shard_map/btd,de->bte/dot_general | solution.py:61
  204.9 5.2 %fusion.70 = bf16[768,640]{1,0:T(8,128)(2,1)S(1)} fusion(bf16[2,2560,640]{2,1,0:T(8,128)(2,1)} %param.18, bf16[1,768,2560]{2,1,0:T(8,128)(2,1)S(1)} %copy-done.3, f32[2560]{0:T(1024)S(1)} %copy-done.17, f32[768]{0:T(1024)S(1)} %add_rsqrt_fusion), kind=kOutput, calls=%fused_computation.90 | convolution fusion | flops 2524938240 | bytes 8205312 | tf_op jit(solution)/shard_map/btd,de->bte/dot_general | solution.py:60
  211.8 0.8 fusion.137
  212.6 2.1 divide_multiply_fusion
  214.7 1.3 copy-done.4
  215.9 1.8 copy.100
  217.8 3.1 reshape_reshape.7
  220.9 1.8 fusion.141
  222.7 1.1 broadcast_multiply_fusion
  223.8 2.0 fusion.58
  225.8 2.9 convolution_bitcast_fusion.2
  228.7 9.1 %fusion.8 = f32[3,10,64,256]{3,2,1,0:T(8,128)S(1)} fusion(f32[3,256,256]{2,1,0:T(8,128)S(1)} %fusion.141, f32[3,10,256]{2,1,0:T(8,128)S(1)} %copy-done.12, pred[256,256]{1,0:T(8,128)(4,1)S(1)} %copy-done.11, f32[3,256,10,64]{1,0,3,2:T(4,128)S(1)} %get-tuple-element.22), kind=kOutput, calls=%fused_computation.14 | convolution fusion | flops 1517813760 | bytes 4814848 | tf_op jit(solution)/shard_map/bchij,bcjhp->bcihp/dot_general | solution.py:37
  237.9 1.9 bitcast_add_fusion
  239.7 1.4 copy.119
  241.1 1.7 copy.143
  242.8 3.1 copy.120
  245.9 8.5 %multiply_reduce_fusion = (f32[768]{0:T(1024)S(1)}, f32[768,640]{1,0:T(8,128)}) fusion(bf16[2,2560,640]{2,1,0:T(8,128)(2,1)} %param.17, bf16[1,768,2560]{2,1,0:T(8,128)(2,1)} %copy-done.2, f32[2560]{0:T(1024)S(1)} %copy-done.18, f32[768]{0:T(1024)S(1)} %copy-done.29, f32[768,640]{1,0:T(8,128)} %copy.120, f32[1,768,640]{2,1,0:T(8,128)S(1)} %copy-done.5, ...), kind=kOutput, calls=%fused_computation.83 | convolution fusion | flops 2529852672 | bytes 13126144 | tf_op jit(solution)/shard_map/btd,de->bte/dot_general | solution.py:59
  254.5 13.0 %psum.30 = f32[1,768,1]{1,2,0:T(1,128)S(1)} all-reduce(f32[1,768,1]{1,2,0:T(1,128)S(1)} %broadcast_in_dim.25), channel_id=1, replica_groups=mesh['dp'=4,'tp'=8] {'tp'}, use_global_device_ids=true, to_apply=%region_12.13 | all-reduce | flops 768 | bytes 6144 | tf_op jit(solution)/shard_map/psum | solution.py:71
  267.5 8.9 %convolution_bitcast_fusion = f32[1,768,2560]{2,1,0:T(8,128)} fusion(bf16[2,640,2560]{2,1,0:T(8,128)(2,1)} %param.29, f32[768,640]{1,0:T(8,128)} %get-tuple-element.62, f32[640]{0:T(1024)S(1)} %copy-done.25, f32[768]{0:T(1024)S(1)} %rsqrt_reduce_fusion), kind=kOutput, calls=%fused_computation.26 | convolution fusion | flops 2518056960 | bytes 13112832 | tf_op jit(solution)/shard_map/bte,ed->btd/dot_general | solution.py:73
  276.5 92.0 %all-reduce.9.cloned.1.call-done = f32[1,768,2560]{2,1,0:T(8,128)} async-done(((f32[1,768,2560]{2,1,0:T(8,128)}), f32[1,768,2560]{2,1,0:T(8,128)}) %all-reduce.9.cloned.1.call-update) | async-done | bytes 7864336 | tf_op jit(solution)/shard_map/psum | solution.py:74
  368.5 7.5 %fusion.7 = bf16[1,768,2560]{2,1,0:T(8,128)(2,1)} fusion(f32[1,768,2560]{2,1,0:T(8,128)} %all-reduce.9.cloned.1.call-done, bf16[1,768,2560]{2,1,0:T(8,128)(2,1)} %copy-done.2), kind=kLoop, calls=%fused_computation.13 | loop fusion | flops 5898240 | bytes 15728640 | tf_op jit(solution)/shard_map/convert_element_type | solution.py:75
  (168 shorter events, 13.6 us)
Async XLA Ops:
  6.5 4.3 %copy-start.14 = (bf16[2,2560]{1,0:T(2,128)(2,1)S(1)}, bf16[2,2560]{1,0:T(2,128)(2,1)}, u32[]{:S(2)}) copy-start(bf16[2,2560]{1,0:T(2,128)(2,1)} %param.16) | copy-start | bytes 30724
  6.5 4.9 %copy-start.9 = (bf16[2,2560,10]{1,0,2:T(2,128)(2,1)S(1)}, bf16[2,2560,10]{1,0,2:T(2,128)(2,1)}, u32[]{:S(2)}) copy-start(bf16[2,2560,10]{1,0,2:T(2,128)(2,1)} %param.20) | copy-start | bytes 307204
  6.6 5.7 %copy-start.41 = (f32[2,10]{1,0:T(2,128)S(1)}, f32[2,10]{1,0:T(2,128)}, u32[]{:S(2)}) copy-start(f32[2,10]{1,0:T(2,128)} %param.26) | copy-start | bytes 244
  6.6 5.7 %copy-start.42 = (f32[2,10]{1,0:T(2,128)S(1)}, f32[2,10]{1,0:T(2,128)}, u32[]{:S(2)}) copy-start(f32[2,10]{1,0:T(2,128)} %param.25) | copy-start | bytes 244
  6.6 183.8 %all-reduce.7.cloned.1.call-start = ((), (), s32[]{:S(2)}) async-start(), calls=%async_computation | async-start | bytes 15728640 | tf_op jit(solution)/shard_map/psum | solution.py:74
  6.6 6.2 %copy-start = (bf16[1,768,2560]{2,1,0:T(8,128)(2,1)S(1)}, bf16[1,768,2560]{2,1,0:T(8,128)(2,1)}, u32[]{:S(2)}) copy-start(bf16[1,768,2560]{2,1,0:T(8,128)(2,1)} %param.15) | copy-start | bytes 11796484
  10.8 16.0 %copy-start.26 = (f32[768]{0:T(1024)}, f32[768]{0:T(1024)S(1)}, u32[]{:S(2)}) copy-start(f32[768]{0:T(1024)S(1)} %add_rsqrt_fusion.1) | copy-start | bytes 9220
  11.5 15.4 %copy-start.19 = (f32[2560]{0:T(1024)}, f32[2560]{0:T(1024)S(1)}, u32[]{:S(2)}) copy-start(f32[2560]{0:T(1024)S(1)} %get-tuple-element.14) | copy-start | bytes 30724
  12.9 4.1 %copy-start.40 = (f32[2,10]{1,0:T(2,128)S(1)}, f32[2,10]{1,0:T(2,128)}, u32[]{:S(2)}) copy-start(f32[2,10]{1,0:T(2,128)} %param.27) | copy-start | bytes 244
  12.9 4.7 %copy-start.31 = (bf16[2,256]{1,0:T(2,128)(2,1)S(1)}, bf16[2,256]{1,0:T(2,128)(2,1)}, u32[]{:S(2)}) copy-start(bf16[2,256]{1,0:T(2,128)(2,1)} %param.24) | copy-start | bytes 3076
  12.9 5.9 %copy-start.16 = (bf16[2,4,256]{2,1,0:T(4,128)(2,1)S(1)}, bf16[2,4,256]{2,1,0:T(4,128)(2,1)}, u32[]{:S(2)}) copy-start(bf16[2,4,256]{2,1,0:T(4,128)(2,1)} %param.22) | copy-start | bytes 12292
  12.9 6.5 %copy-start.21 = (bf16[2,640]{1,0:T(2,128)(2,1)S(1)}, bf16[2,640]{1,0:T(2,128)(2,1)}, u32[]{:S(2)}) copy-start(bf16[2,640]{1,0:T(2,128)(2,1)} %param.23) | copy-start | bytes 7684
  12.9 7.1 %copy-start.22 = (bf16[2,640]{1,0:T(2,128)(2,1)S(1)}, bf16[2,640]{1,0:T(2,128)(2,1)}, u32[]{:S(2)}) copy-start(bf16[2,640]{1,0:T(2,128)(2,1)} %param.28) | copy-start | bytes 7684
  12.9 7.7 %copy-start.15 = (bf16[2,4,640]{2,1,0:T(4,128)(2,1)S(1)}, bf16[2,4,640]{2,1,0:T(4,128)(2,1)}, u32[]{:S(2)}) copy-start(bf16[2,4,640]{2,1,0:T(4,128)(2,1)} %param.21) | copy-start | bytes 30724
  22.3 4.5 %copy-start.1 = (bf16[1,768,2560]{2,1,0:T(8,128)(2,1)S(1)}, bf16[1,768,2560]{2,1,0:T(8,128)(2,1)}, u32[]{:S(2)}) copy-start(bf16[1,768,2560]{2,1,0:T(8,128)(2,1)} %param.15) | copy-start | bytes 11796484
  33.4 1.3 copy-start.6
  41.5 2.0 copy-start.38
  41.5 4.9 %copy-start.11 = (pred[256,256]{1,0:T(8,128)(4,1)S(1)}, pred[256,256]{1,0:T(8,128)(4,1)}, u32[]{:S(2)}) copy-start(pred[256,256]{1,0:T(8,128)(4,1)} %iota_compare_fusion) | copy-start | bytes 196612
  41.6 4.9 %copy-start.13 = (f32[3,10,256]{2,1,0:T(8,128)S(1)}, f32[3,10,256]{2,1,0:T(8,128)}, u32[]{:S(2)}) copy-start(f32[3,10,256]{2,1,0:T(8,128)} %copy.84) | copy-start | bytes 92164
  60.7 3.0 copy-start.7
  60.7 3.0 copy-start.20
  60.7 3.0 copy-start.24
  60.7 3.0 copy-start.27
  63.7 22.3 %copy-start.30 = (f32[640]{0:T(1024)S(1)}, f32[640]{0:T(1024)}, u32[]{:S(2)}) copy-start(f32[640]{0:T(1024)} %get-tuple-element.16) | copy-start | bytes 7684
  95.0 0.6 copy-start.37
  95.0 273.5 %all-reduce.9.cloned.1.call-start = ((), (), s32[]{:S(2)}) async-start(), calls=%async_computation.1 | async-start | bytes 15728640 | tf_op jit(solution)/shard_map/psum | solution.py:74
  96.3 99.9 %copy-start.10 = (bf16[1,2560,10]{1,0,2:T(2,128)(2,1)S(1)}, bf16[1,2560,10]{1,0,2:T(2,128)(2,1)}, u32[]{:S(2)}) copy-start(bf16[1,2560,10]{1,0,2:T(2,128)(2,1)} %get-tuple-element.33) | copy-start | bytes 153604
  96.3 99.9 %copy-start.17 = (f32[2560]{0:T(1024)S(1)}, f32[2560]{0:T(1024)}, u32[]{:S(2)}) copy-start(f32[2560]{0:T(1024)} %get-tuple-element.13) | copy-start | bytes 30724
  96.3 99.9 %copy-start.43 = (f32[10]{0:T(128)S(1)}, f32[10]{0:T(128)}, u32[]{:S(2)}) copy-start(f32[10]{0:T(128)} %get-tuple-element.45) | copy-start | bytes 124
  96.3 99.9 %copy-start.44 = (f32[10]{0:T(128)S(1)}, f32[10]{0:T(128)}, u32[]{:S(2)}) copy-start(f32[10]{0:T(128)} %get-tuple-element.64) | copy-start | bytes 124
  196.2 1.9 copy-start.2
  196.2 8.7 %copy-start.28 = (f32[768]{0:T(1024)}, f32[768]{0:T(1024)S(1)}, u32[]{:S(2)}) copy-start(f32[768]{0:T(1024)S(1)} %add_rsqrt_fusion) | copy-start | bytes 9220
  200.9 3.9 %copy-start.3 = (bf16[1,768,2560]{2,1,0:T(8,128)(2,1)S(1)}, bf16[1,768,2560]{2,1,0:T(8,128)(2,1)}, u32[]{:S(2)}) copy-start(bf16[1,768,2560]{2,1,0:T(8,128)(2,1)} %copy-done.2) | copy-start | bytes 11796484
  204.9 6.3 %copy-start.32 = (f32[1,1,256]{2,1,0:T(1,128)S(1)}, f32[1,1,256]{2,1,0:T(1,128)}, u32[]{:S(2)}) copy-start(f32[1,1,256]{2,1,0:T(1,128)} %get-tuple-element.35) | copy-start | bytes 3076
  204.9 6.3 %copy-start.33 = (f32[1,1,256]{2,1,0:T(1,128)S(1)}, f32[1,1,256]{2,1,0:T(1,128)}, u32[]{:S(2)}) copy-start(f32[1,1,256]{2,1,0:T(1,128)} %get-tuple-element.36) | copy-start | bytes 3076
  204.9 6.3 %copy-start.34 = (f32[1,1,256]{2,1,0:T(1,128)S(1)}, f32[1,1,256]{2,1,0:T(1,128)}, u32[]{:S(2)}) copy-start(f32[1,1,256]{2,1,0:T(1,128)} %get-tuple-element.41) | copy-start | bytes 3076
  204.9 6.3 %copy-start.35 = (f32[1,1,256]{2,1,0:T(1,128)S(1)}, f32[1,1,256]{2,1,0:T(1,128)}, u32[]{:S(2)}) copy-start(f32[1,1,256]{2,1,0:T(1,128)} %get-tuple-element.42) | copy-start | bytes 3076
  204.9 6.3 %copy-start.36 = (f32[1,256]{1,0:T(1,128)S(1)}, f32[1,256]{1,0:T(1,128)}, u32[]{:S(2)}) copy-start(f32[1,256]{1,0:T(1,128)} %get-tuple-element.49) | copy-start | bytes 3076
  214.7 1.3 copy-start.4
  223.8 2.0 copy-start.39
  223.8 4.9 %copy-start.12 = (f32[3,10,256]{2,1,0:T(8,128)S(1)}, f32[3,10,256]{2,1,0:T(8,128)}, u32[]{:S(2)}) copy-start(f32[3,10,256]{2,1,0:T(8,128)} %copy.106) | copy-start | bytes 92164
  228.7 9.2 %copy-start.8 = (f32[1,768,128]{2,1,0:T(8,128)S(1)}, f32[1,768,128]{2,1,0:T(8,128)}, u32[]{:S(2)}) copy-start(f32[1,768,128]{2,1,0:T(8,128)} %get-tuple-element.30) | copy-start | bytes 1179652
  242.8 3.1 copy-start.5
  242.8 3.1 copy-start.18
  242.8 3.1 copy-start.23
  242.8 3.1 copy-start.29
  245.9 21.6 %copy-start.25 = (f32[640]{0:T(1024)S(1)}, f32[640]{0:T(1024)}, u32[]{:S(2)}) copy-start(f32[640]{0:T(1024)} %get-tuple-element.15) | copy-start | bytes 7684
Sparse Core Ops, SparseCore 0:
  95.1 95.1 all-reduce.6
  276.6 91.8 all-reduce.8
where the time goes:
time: 391 us; the launch traced here: 383 us
  waiting for transfers between devices  186 us (48%)
  matrix products  89.7 us (23%)
  local copies, waits for them, and re-layouts  33.6 us (9%)
  other arithmetic  31.8 us (8%)
  blocking collectives  26.9 us (7%)
  between operations  14.9 us (4%)
    psum x2, waiting for transfers between devices, mixer_layer(): full_out = lax.psum(part_out, 'tp')  186 us
    psum x2, blocking collectives, mixer_layer(): total_sq = lax.psum(part_sq, 'tp')  26.9 us
    dot_general x2, matrix products, ssd_blocks(): jnp.einsum('bchij,bcjhp->bcihp', mix_mat, x_dt, precision=FULL_PRECISION)  18.4 us
    dot_general x2, matrix products, mixer_layer(): jnp.einsum('bte,ed->btd', normed_y, w_out, preferred_element_type=jnp.flo...  17.8 us
    dot_general x2, matrix products, mixer_layer(): jnp.einsum('btd,de->bte', normed, w_z, preferred_element_type=jnp.float32)  16.9 us
    dot_general x2, matrix products, mixer_layer(): jnp.einsum('btd,de->bte', normed, w_x, preferred_element_type=jnp.float32)  10.4 us
    reduce_sum x2, other arithmetic, mixer_layer(): jnp.mean(residual * residual, axis=-1, keepdims=True) + EPSILON  8.75 us
  transfers between devices with their start and end apart: 2, of which 2 were waited for; matrix products, arithmetic and copies ran while one was open for 0% of the time, Pallas kernels for 0%

commit v1 on v0

v1 whole, which is shorter than its diff:
```python
import functools

import jax
import jax.numpy as jnp
from jax import lax
from jax.experimental import pallas as pl
from jax.experimental.pallas import tpu as pltpu
from jax.sharding import PartitionSpec as P

EPSILON = 1e-5
F32 = jnp.float32
BF16 = jnp.bfloat16
FULL = lax.Precision.HIGHEST
MESH = pl.DeviceIdType.MESH
LANES = 128
CHUNK = 128
SLOTS = 4
HALO = 8
SIB, FAR_P, FAR_M, NEAR_P, NEAR_M, COMB_P, COMB_M, AG_P, AG_M, FW_P, FW_M, D0, D1, D2, D3 = range(15)


def full_dot(a, b, dims=(((1,), (0,)), ((), ()))):
    return lax.dot_general(a, b, dims, precision=FULL, preferred_element_type=F32)


def silu(a):
    return a * (1.0 / (1.0 + jnp.exp(-a)))


def softplus(a):
    return jnp.maximum(a, 0.0) + jnp.log1p(jnp.exp(-jnp.abs(a)))


def kernel(tp_size, conv_width, hid_hbm, norm_in, wz_hbm, wx_hbm, wbc_hbm, wdt_hbm, convx_in, convbc_in, biasx_in, biasbc_in,
           dtb_in, alog_in, dskip_in, gate_in, wout_hbm, out_hbm,
           hid, win, wdt, wout, ures, h, pre, act, v, g, dtp, state, pbuf, sib, far, near, comb, stats, nw, cw, gw, hp, ost,
           wsem, hsem, osem, ssend, srecv, msend, mrecv):
    n_layers, n_steps, d_model = ures.shape
    width = v.shape[1]
    conv_ch = act.shape[1]
    n_state = (conv_ch - width) // 2
    n_heads = dtb_in.shape[1]
    head_dim = width // n_heads
    n_chunks = n_steps // CHUNK
    n_tasks = n_layers * n_chunks
    n_chips = tp_size // 2
    half_rows = CHUNK // 2
    slice_rows = half_rows // n_chips
    piece = slice_rows // 2
    inner_width = width * tp_size

    me = lax.axis_index('tp')
    chip = me // 2
    core = lax.rem(me, 2)
    nxt = lax.rem(chip + 1, n_chips)
    prv = lax.rem(chip + n_chips - 1, n_chips)
    opp = lax.rem(chip + 2, n_chips)
    dev_nxt = {'tp': nxt * 2 + core}
    dev_prv = {'tp': prv * 2 + core}
    dev_sib = {'tp': chip * 2 + 1 - core}

    barrier = pltpu.get_barrier_semaphore()
    for off in range(1, tp_size):
        pl.semaphore_signal(barrier, inc=1, device_id={'tp': lax.rem(me + off, tp_size)}, device_id_type=MESH)

    def load_hid(i):
        rows = pl.ds(pl.multiple_of(i * CHUNK, CHUNK), CHUNK)
        return pltpu.make_async_copy(hid_hbm.at[rows], hid.at[rows], hsem.at[i])

    def load_in(layer):
        return (
            pltpu.make_async_copy(wz_hbm.at[layer], win.at[layer, :, pl.ds(0, width)], wsem.at[layer, 0]),
            pltpu.make_async_copy(wx_hbm.at[layer], win.at[layer, :, pl.ds(width, width)], wsem.at[layer, 1]),
            pltpu.make_async_copy(wbc_hbm.at[layer], win.at[layer, :, pl.ds(2 * width, 2 * n_state)], wsem.at[layer, 2]),
            pltpu.make_async_copy(wdt_hbm.at[layer], wdt.at[layer], wsem.at[layer, 3]),
        )

    def load_out(layer):
        return pltpu.make_async_copy(wout_hbm.at[layer], wout.at[layer], wsem.at[layer, 4])

    load_hid(0).start()
    for layer in range(n_layers):
        for cp in load_in(layer):
            cp.start()
        load_out(layer).start()
        if layer == 0:
            for i in range(1, n_chunks):
                load_hid(i).start()

    hp[...] = jnp.zeros_like(hp)
    dtp[...] = jnp.zeros_like(dtp)
    for layer in range(n_layers):
        nw[layer, 0:1, :] = norm_in[layer:layer + 1, :].astype(F32)
        gw[layer, 0:1, :] = gate_in[layer:layer + 1, :].astype(F32)
        cw[layer, 0:conv_width, 0:width] = convx_in[layer].astype(F32)
        cw[layer, 0:conv_width, width:conv_ch] = convbc_in[layer].astype(F32)
        cw[layer, conv_width:conv_width + 1, 0:width] = biasx_in[layer:layer + 1, :].astype(F32)
        cw[layer, conv_width:conv_width + 1, width:conv_ch] = biasbc_in[layer:layer + 1, :].astype(F32)
        hp[layer, 0:1, 0:n_heads] = dtb_in[layer:layer + 1, :]
        hp[layer, 1:2, 0:n_heads] = alog_in[layer:layer + 1, :]
        hp[layer, 2:3, 0:n_heads] = dskip_in[layer:layer + 1, :]

    pl.semaphore_wait(barrier, tp_size - 1)

    def where_of(t):
        layer = t // n_chunks
        return layer, pl.multiple_of((t - layer * n_chunks) * CHUNK, CHUNK)

    def remote(src, dst, slot, kind, dev):
        return pltpu.make_async_remote_copy(src_ref=src, dst_ref=dst, send_sem=msend.at[slot, kind], recv_sem=mrecv.at[slot, kind],
                                            device_id=dev, device_id_type=MESH)

    def slice_at(c, j):
        return pl.multiple_of(c * half_rows + j * slice_rows, slice_rows)

    def msg_rs(t, kind):
        slot = lax.rem(t, SLOTS)
        buf = pbuf.at[lax.rem(t, 2)]

        def src(j, part):
            return buf.at[pl.ds(pl.multiple_of(slice_at(core, j) + part * piece, piece), piece)]
        if kind == SIB:
            other = pl.multiple_of((1 - core) * half_rows, half_rows)
            return remote(buf.at[pl.ds(other, half_rows)], sib.at[lax.rem(t, 2)], slot, kind, dev_sib)
        if kind == FAR_P:
            return remote(src(opp, 1), far.at[slot, 0], slot, kind, dev_nxt)
        if kind == FAR_M:
            return remote(src(opp, 0), far.at[slot, 1], slot, kind, dev_prv)
        if kind == NEAR_P:
            return remote(src(nxt, 0), near.at[slot, 0], slot, kind, dev_nxt)
        if kind == NEAR_M:
            return remote(src(prv, 1), near.at[slot, 1], slot, kind, dev_prv)
        if kind == COMB_P:
            return remote(src(nxt, 1), comb.at[slot, 0], slot, kind, dev_nxt)
        return remote(src(prv, 0), comb.at[slot, 1], slot, kind, dev_prv)

    def msg_ag(t, kind, c=None):
        slot = lax.rem(t, SLOTS)
        layer, row0 = where_of(t)
        c = core if c is None else c

        def rows(j, part=None):
            base = row0 + slice_at(c, j)
            if part is None:
                return ures.at[layer, pl.ds(pl.multiple_of(base, slice_rows), slice_rows)]
            return ures.at[layer, pl.ds(pl.multiple_of(base + part * piece, piece), piece)]
        ref, dev = {
            AG_P: lambda: (rows(chip), dev_nxt),
            AG_M: lambda: (rows(chip), dev_prv),
            FW_P: lambda: (rows(prv, 0), dev_nxt),
            FW_M: lambda: (rows(nxt, 1), dev_prv),
            D0: lambda: (rows(chip), dev_sib),
            D1: lambda: (rows(prv), dev_sib),
            D2: lambda: (rows(nxt), dev_sib),
            D3: lambda: (rows(opp), dev_sib),
        }[kind]()
        return remote(ref, ref, slot, kind, dev)

    def wait_ag(t, kind):
        slot = lax.rem(t, SLOTS)
        layer, row0 = where_of(t)

        def rows(c, j, part=None):
            base = row0 + slice_at(c, j)
            if part is None:
                return ures.at[layer, pl.ds(pl.multiple_of(base, slice_rows), slice_rows)]
            return ures.at[layer, pl.ds(pl.multiple_of(base + part * piece, piece), piece)]
        ref = {
            AG_P: lambda: rows(core, prv),
            AG_M: lambda: rows(core, nxt),
            FW_P: lambda: rows(core, opp, 0),
            FW_M: lambda: rows(core, opp, 1),
            D0: lambda: rows(1 - core, chip),
            D1: lambda: rows(1 - core, prv),
            D2: lambda: rows(1 - core, nxt),
            D3: lambda: rows(1 - core, opp),
        }[kind]()
        remote(ref, ref, slot, kind, dev_sib).wait_recv()

    def msg_stat(t, off):
        slot = lax.rem(t, SLOTS)
        return pltpu.make_async_remote_copy(src_ref=stats.at[slot, me], dst_ref=stats.at[slot, me], send_sem=ssend.at[slot, off],
                                            recv_sem=srecv.at[slot, me], device_id={'tp': lax.rem(me + off, tp_size)}, device_id_type=MESH)

    def in_proj(t):
        layer, row0 = where_of(t)

        @pl.when(layer == 0)
        def _():
            load_hid(t).wait()

        @pl.when(row0 == 0)
        def _():
            for cp in load_in(layer):
                cp.wait()
            pre[0:HALO, :] = jnp.zeros((HALO, pre.shape[1]), F32)

        @pl.when(row0 > 0)
        def _():
            pre[0:HALO, :] = pre[CHUNK:CHUNK + HALO, :]

        def norm(load):
            def block(i, carry):
                r = pl.multiple_of(i * 16, 16)
                u = load(pl.multiple_of(row0 + r, 16))
                scale = lax.rsqrt(jnp.mean(u * u, axis=-1, keepdims=True) + EPSILON)
                h[pl.ds(r, 16), :] = (u * scale * nw[layer, 0:1, :]).astype(BF16)
                return carry
            lax.fori_loop(0, CHUNK // 16, block, 0)

        @pl.when(layer == 0)
        def _():
            norm(lambda r: hid[pl.ds(r, 16), :].astype(F32))

        @pl.when(layer > 0)
        def _():
            norm(lambda r: ures[jnp.maximum(layer - 1, 0), pl.ds(r, 16), :])

        def tile(i, carry):
            o = pl.multiple_of(i * 256, 256)
            prod = jnp.dot(h[...], win[layer, :, pl.ds(o, 256)], preferred_element_type=F32)
            pre[HALO:HALO + CHUNK, pl.ds(o, 256)] = prod.astype(BF16).astype(F32)
            return carry
        lax.fori_loop(0, pre.shape[1] // 256, tile, 0)
        prod = jnp.dot(h[...], wdt[layer], preferred_element_type=F32)
        dtp[:, 0:n_heads] = prod.astype(BF16).astype(F32)

    def mix(t):
        slot = lax.rem(t, SLOTS)
        layer, row0 = where_of(t)

        @pl.when(row0 == 0)
        def _():
            state[...] = jnp.zeros_like(state)

        def conv(i, carry):
            o = pl.multiple_of(i * LANES, LANES)
            acc = jnp.broadcast_to(cw[layer, conv_width:conv_width + 1, pl.ds(o, LANES)], (CHUNK, LANES))
            for j in range(conv_width):
                first = HALO - (conv_width - 1) + j
                acc = acc + pre[first:first + CHUNK, pl.ds(pl.multiple_of(width + o, LANES), LANES)] * cw[layer, j:j + 1, pl.ds(o, LANES)]
            act[:, pl.ds(o, LANES)] = silu(acc)
            return carry
        lax.fori_loop(0, conv_ch // LANES, conv, 0)

        row_id = lax.broadcasted_iota(jnp.int32, (CHUNK, CHUNK), 0)
        col_id = lax.broadcasted_iota(jnp.int32, (CHUNK, CHUNK), 1)
        lower = row_id >= col_id
        left = col_id < head_dim
        left_row = left[0:1, :]
        dt = softplus(dtp[...] + hp[layer, 0:1, :])
        a = -dt * jnp.exp(hp[layer, 1:2, :])
        a_cum = full_dot(jnp.where(lower, 1.0, 0.0).astype(F32), a)
        a_cum_t = a_cum.T
        a_last = a_cum[CHUNK - 1:CHUNK, :]
        from_start = jnp.exp(a_cum)
        to_end = jnp.exp(a_last - a_cum)
        whole = jnp.exp(a_last)
        skip = hp[layer, 2:3, :]
        b = act[:, width:width + n_state]
        c = act[:, width + n_state:conv_ch]
        c_dot_b = full_dot(c, b, (((1,), (1,)), ((), ())))
        b_t = b.T
        sq = jnp.zeros((CHUNK, LANES), F32)
        for p in range(width // LANES):
            cols = slice(p * LANES, (p + 1) * LANES)
            h0, h1 = 2 * p, 2 * p + 1

            def spread(m):
                return jnp.where(left, m[:, h0:h0 + 1], m[:, h1:h1 + 1])

            def spread_row(m):
                return jnp.where(left_row, m[:, h0:h0 + 1], m[:, h1:h1 + 1])

            def mixer(n):
                seg = a_cum[:, n:n + 1] - a_cum_t[n:n + 1, :]
                return jnp.where(lower, jnp.exp(jnp.minimum(seg, 0.0)), 0.0) * c_dot_b
            x = act[:, cols]
            x_dt = x * spread(dt)
            both = jnp.concatenate([jnp.where(left, x_dt, 0.0), jnp.where(left, 0.0, x_dt)], axis=0)
            y = full_dot(jnp.concatenate([mixer(h0), mixer(h1)], axis=1), both)
            s_in = state[:, cols]
            y = y + full_dot(c, s_in) * spread(from_start)
            state[:, cols] = s_in * spread_row(whole) + full_dot(b_t, x_dt * spread(to_end))
            y = y + spread_row(skip) * x
            gated = y * silu(pre[HALO:HALO + CHUNK, cols])
            v[:, cols] = gated
            sq = sq + gated * gated
        total = jnp.sum(sq.T, axis=0, keepdims=True)
        stats[slot, me] = jnp.broadcast_to(total, (8, CHUNK))
        for off in range(1, tp_size):
            msg_stat(t, off).start()

    def out_proj(t):
        slot = lax.rem(t, SLOTS)
        layer, row0 = where_of(t)

        @pl.when(row0 == 0)
        def _():
            load_out(layer).wait()
        for off in range(1, tp_size):
            peer = lax.rem(me + off, tp_size)
            pltpu.make_async_remote_copy(src_ref=stats.at[slot, peer], dst_ref=stats.at[slot, peer], send_sem=ssend.at[slot, off],
                                         recv_sem=srecv.at[slot, peer], device_id=dev_sib, device_id_type=MESH).wait_recv()
        for off in range(1, tp_size):
            msg_stat(t, off).wait_send()
        total = stats[slot, 0]
        for r in range(1, tp_size):
            total = total + stats[slot, r]
        scale = lax.rsqrt(total / inner_width + EPSILON)
        scale = jnp.broadcast_to(scale[0:1, :], (LANES, CHUNK)).T
        for p in range(width // LANES):
            cols = slice(p * LANES, (p + 1) * LANES)
            g[:, cols] = (v[:, cols] * scale * gw[layer, 0:1, cols]).astype(BF16)
        buf = pbuf.at[lax.rem(t, 2)]

        def tile(i, carry):
            o = pl.multiple_of(i * 256, 256)
            buf[:, pl.ds(o, 256)] = jnp.dot(g[...], wout[layer, :, pl.ds(o, 256)], preferred_element_type=F32)
            return carry
        lax.fori_loop(0, d_model // 256, tile, 0)
        msg_rs(t, SIB).start()

    def pair_sum(t):
        msg_rs(t, SIB).wait_recv()
        buf, other = pbuf.at[lax.rem(t, 2)], sib.at[lax.rem(t, 2)]

        def block(i, carry):
            r = pl.multiple_of(i * 8, 8)
            mine = pl.ds(pl.multiple_of(core * half_rows + r, 8), 8)
            buf[mine, :] = buf[mine, :] + other[pl.ds(r, 8), :]
            return carry
        lax.fori_loop(0, half_rows // 8, block, 0)
        for kind in (FAR_P, FAR_M, NEAR_P, NEAR_M):
            msg_rs(t, kind).start()

    def relay_sum(t):
        slot = lax.rem(t, SLOTS)
        buf = pbuf.at[lax.rem(t, 2)]
        for way, (wait, send, j, part) in enumerate(((FAR_P, COMB_P, nxt, 1), (FAR_M, COMB_M, prv, 0))):
            msg_rs(t, wait).wait_recv()
            rows = pl.ds(pl.multiple_of(slice_at(core, j) + part * piece, piece), piece)
            buf[rows, :] = buf[rows, :] + far[slot, way]
            msg_rs(t, send).start()

    def finish(t):
        slot = lax.rem(t, SLOTS)
        layer, row0 = where_of(t)
        buf = pbuf.at[lax.rem(t, 2)]
        for kind in (NEAR_P, NEAR_M, COMB_P, COMB_M):
            msg_rs(t, kind).wait_recv()
        base = slice_at(core, chip)
        dst = pl.ds(pl.multiple_of(row0 + base, slice_rows), slice_rows)

        def store(res):
            lo = buf[pl.ds(base, piece), :] + near[slot, 0] + comb[slot, 1]
            hi = buf[pl.ds(pl.multiple_of(base + piece, piece), piece), :] + near[slot, 1] + comb[slot, 0]
            ures[layer, dst, :] = (res + jnp.concatenate([lo, hi], axis=0)).astype(BF16).astype(F32)

        @pl.when(layer == 0)
        def _():
            store(hid[dst, :].astype(F32))

        @pl.when(layer > 0)
        def _():
            store(ures[jnp.maximum(layer - 1, 0), dst, :])
        for kind in (AG_P, AG_M, D0):
            msg_ag(t, kind).start()
        for kind in (SIB, FAR_P, FAR_M, NEAR_P, NEAR_M, COMB_P, COMB_M):
            msg_rs(t, kind).wait_send()

    def forward(t):
        wait_ag(t, AG_P)
        msg_ag(t, FW_P).start()
        wait_ag(t, AG_M)
        msg_ag(t, FW_M).start()
        msg_ag(t, D1).start()
        msg_ag(t, D2).start()

    def collect(t):
        layer, row0 = where_of(t)
        wait_ag(t, FW_P)
        wait_ag(t, FW_M)
        msg_ag(t, D3).start()
        for kind in (D0, D1, D2, D3):
            wait_ag(t, kind)
        for kind in (AG_P, AG_M, FW_P, FW_M, D0, D1, D2, D3):
            msg_ag(t, kind).wait_send()

        @pl.when(layer == n_layers - 1)
        def _():
            rows = pl.ds(row0, CHUNK)

            def block(i, carry):
                r = pl.multiple_of(i * 16, 16)
                ost[pl.ds(r, 16), :] = ures[layer, pl.ds(pl.multiple_of(row0 + r, 16), 16), :].astype(BF16)
                return carry

            @pl.when(row0 > 0)
            def _():
                pltpu.make_async_copy(ost, out_hbm.at[rows], osem).wait()
            lax.fori_loop(0, CHUNK // 16, block, 0)
            pltpu.make_async_copy(ost, out_hbm.at[rows], osem).start()

    def guarded(step, t):
        @pl.when((t >= 0) & (t < n_tasks))
        def _():
            step(t)

    def iteration(t, carry):
        guarded(mix, t)
        guarded(forward, t - 3)
        guarded(pair_sum, t - 1)
        guarded(finish, t - 2)
        guarded(in_proj, t + 1)
        guarded(relay_sum, t - 1)
        guarded(out_proj, t)
        guarded(collect, t - 4)
        return carry
    lax.fori_loop(-1, n_tasks + 4, iteration, 0)
    pltpu.make_async_copy(ost, out_hbm.at[pl.ds(0, CHUNK)], osem).wait()


def layers(tp_size, hidden, norm_w, w_z, w_x, w_bc, w_dt, conv_x, conv_bc, bias_x, bias_bc, dt_bias, a_log, d_skip, gate_w, w_out):
    n_batch, n_steps, d_model = hidden.shape
    n_layers, conv_width, width = conv_x.shape
    n_heads = dt_bias.shape[-1]
    state2 = w_bc.shape[-1]
    piece = CHUNK // tp_size // 2
    any_spec = pl.BlockSpec(memory_space=pl.ANY)
    vmem_spec = pl.BlockSpec(memory_space=pltpu.VMEM)
    dma = pltpu.SemaphoreType.DMA
    run = pl.pallas_call(
        functools.partial(kernel, tp_size, conv_width),
        out_shape=jax.ShapeDtypeStruct((n_steps, d_model), BF16),
        in_specs=[any_spec, vmem_spec, any_spec, any_spec, any_spec, any_spec] + [vmem_spec] * 8 + [any_spec],
        out_specs=any_spec,
        scratch_shapes=[
            pltpu.VMEM((n_steps, d_model), BF16),
            pltpu.VMEM((n_layers, d_model, 2 * width + state2), BF16),
            pltpu.VMEM((n_layers, d_model, n_heads), BF16),
            pltpu.VMEM((n_layers, width, d_model), BF16),
            pltpu.VMEM((n_layers, n_steps, d_model), F32),
            pltpu.VMEM((CHUNK, d_model), BF16),
            pltpu.VMEM((HALO + CHUNK, 2 * width + state2), F32),
            pltpu.VMEM((CHUNK, width + state2), F32),
            pltpu.VMEM((CHUNK, width), F32),
            pltpu.VMEM((CHUNK, width), BF16),
            pltpu.VMEM((CHUNK, LANES), F32),
            pltpu.VMEM((state2 // 2, width), F32),
            pltpu.VMEM((2, CHUNK, d_model), F32),
            pltpu.VMEM((2, CHUNK // 2, d_model), F32),
            pltpu.VMEM((SLOTS, 2, piece, d_model), F32),
            pltpu.VMEM((SLOTS, 2, piece, d_model), F32),
            pltpu.VMEM((SLOTS, 2, piece, d_model), F32),
            pltpu.VMEM((SLOTS, tp_size, 8, CHUNK), F32),
            pltpu.VMEM((n_layers, 8, d_model), F32),
            pltpu.VMEM((n_layers, 8, width + state2), F32),
            pltpu.VMEM((n_layers, 8, width), F32),
            pltpu.VMEM((n_layers, 8, LANES), F32),
            pltpu.VMEM((CHUNK, d_model), BF16),
            dma((n_layers, 5)), dma((n_steps // CHUNK,)), dma,
            dma((SLOTS, tp_size)), dma((SLOTS, tp_size)), dma((SLOTS, 15)), dma((SLOTS, 15)),
        ],
        compiler_params=pltpu.CompilerParams(collective_id=0, has_side_effects=True, vmem_limit_bytes=67_043_328),
    )
    outs = [run(hidden[i], norm_w, w_z, w_x, w_bc, w_dt, conv_x, conv_bc, bias_x, bias_bc, dt_bias, a_log, d_skip, gate_w, w_out)
            for i in range(n_batch)]
    return jnp.stack(outs)


def solution(mesh):
    col_spec = P(None, None, 'tp')
    vec_spec = P(None, 'tp')
    in_specs = (P('dp'), P(), col_spec, col_spec, P(), col_spec, col_spec, P(), vec_spec, P(), vec_spec, vec_spec, vec_spec, vec_spec, P(None, 'tp', None))
    return jax.shard_map(functools.partial(layers, mesh.shape['tp']), mesh=mesh, in_specs=in_specs, out_specs=P('dp'), check_vma=False)
```

time: 391 us -> 193 us (0.49); the launches traced: 383 us -> 193 us
  Pallas kernels: 0 us -> 187 us
  waiting for transfers between devices: 186 us -> 0 us
  matrix products: 89.7 us -> 0 us
  other arithmetic: 31.8 us -> 0 us
  local copies, waits for them, and re-layouts: 33.6 us -> 6.53 us
  blocking collectives: 26.9 us -> 0 us
  between operations: 14.9 us -> 0.01 us
    pallas_call x0 -> x1, Pallas kernels: none -> 187 us  [layers(): run(hidden[i], norm_w, w_z, w_x, w_bc, w_dt, conv_x, conv_bc, bias_x, bia...]
    psum x2 -> x0, waiting for transfers between devices: 186 us -> none  [mixer_layer(): full_out = lax.psum(part_out, 'tp')]
    dot_general x20 -> x0, matrix products: 89.7 us -> none  [the longest x2 18.4 us: ssd_blocks(): jnp.einsum('bchij,bcjhp->bcihp', mix_mat, x_dt, precision=FULL_PRECISION)]
    psum x2 -> x0, blocking collectives: 26.9 us -> none  [mixer_layer(): total_sq = lax.psum(part_sq, 'tp')]
    convert_element_type x5 -> x0, other arithmetic: 9.85 us -> none  [the longest x1 7.49 us: mixer_layer(): return (residual + full_out).astype(jnp.bfloat16)]
    reduce_sum x2 -> x0, other arithmetic: 8.75 us -> none  [mixer_layer(): jnp.mean(residual * residual, axis=-1, keepdims=True) + EPSILON]
    another operation x23 -> x0, local copies, waits for them, and re-layouts: 8.52 us -> none  [the longest x2 6.26 us: ssd_blocks(): x_heads.reshape(n_batch, n_blocks, BLOCK_LEN, n_heads, head_width)]
    mul x8 -> x0, other arithmetic: 7.97 us -> none  [the longest x2 3.4 us: mixer_layer(): x_act = jax.nn.silu(causal_conv(x_pre, conv_x, bias_x))]
  transfers between devices with their start and end apart: 2 -> 0, of which waited for: 2 -> 0; matrix products, arithmetic and copies ran while one was open for 0% -> 0% of each run, Pallas kernels for 0% -> 0%
where the time goes in v1:
time: 193 us
  Pallas kernels  187 us (97%)
  local copies, waits for them, and re-layouts  6.53 us (3%)
    pallas_call x1, Pallas kernels, layers(): run(hidden[i], norm_w, w_z, w_x, w_bc, w_dt, conv_x, conv_bc, bias_x, bia...  187 us
    unnamed x2, local copies, waits for them, and re-layouts  6.53 us

profile of v1, /device:TPU:81, one launch (start us, length us, event | category | flops | bytes accessed | tf_op | source)
XLA Modules:
  0.0 193.0 jit_solution(2267602658914690088)
XLA Ops:
  0.0 2.2 %copy.16.wdt_hbm = bf16[2,2560,10]{2,1,0:T(8,128)(2,1)} copy(bf16[2,2560,10]{1,0,2:T(2,128)(2,1)} %param.20) | data formatting | bytes 204800 | tf_op args[5]
  2.2 186.5 %shard_map.145 = bf16[768,2560]{1,0:T(8,128)(2,1)} custom-call(bf16[768,2560]{1,0:T(8,128)(2,1)} %bitcast.3, bf16[2,2560]{1,0:T(2,128)(2,1)} %norm_in.1, bf16[2,2560,640]{2,1,0:T(8,128)(2,1)} %wz_hbm.1, bf16[2,2560,640]{2,1,0:T(8,128)(2,1)} %wx_hbm.1, bf16[2,2560,256]{2,1,0:T(8,128)(2,1)} %wbc_hbm.1, bf16[2,2560,10]{2,1,0:T(8,128)(2,1)} %copy.16.wdt_hbm, ...), custom_call_target="tpu_custom_call" | custom-call | tf_op jit(solution)/shard_map/pallas_call | solution.py:467
  188.8 4.3 %copy.18 = bf16[1,768,2560]{2,1,0:T(8,128)(2,1)} copy(bf16[1,768,2560]{2,1,0:T(8,128)(2,1)} %bitcast.2) | data formatting | bytes 7864320

commit v2 on v1

--- a/solution.py
+++ b/solution.py
@@ -16,6 +16,7 @@
 CHUNK = 128
 SLOTS = 4
 HALO = 8
+TILE = 256
 SIB, FAR_P, FAR_M, NEAR_P, NEAR_M, COMB_P, COMB_M, AG_P, AG_M, FW_P, FW_M, D0, D1, D2, D3 = range(15)
 
 
@@ -31,10 +32,11 @@
     return jnp.maximum(a, 0.0) + jnp.log1p(jnp.exp(-jnp.abs(a)))
 
 
-def kernel(tp_size, conv_width, hid_hbm, norm_in, wz_hbm, wx_hbm, wbc_hbm, wdt_hbm, convx_in, convbc_in, biasx_in, biasbc_in,
-           dtb_in, alog_in, dskip_in, gate_in, wout_hbm, out_hbm,
-           hid, win, wdt, wout, ures, h, pre, act, v, g, dtp, state, pbuf, sib, far, near, comb, stats, nw, cw, gw, hp, ost,
-           wsem, hsem, osem, ssend, srecv, msend, mrecv):
+def kernel(tp_size, conv_width, hid_hbm, norm_hbm, wz_hbm, wx_hbm, wbc_hbm, wdt_hbm, convx_hbm, convbc_hbm, biasx_hbm, biasbc_hbm,
+           dtb_hbm, alog_hbm, dskip_hbm, gate_hbm, wout_hbm, out,
+           norm_in, wdt_in, convx_in, convbc_in, biasx_in, biasbc_in, dtb_in, alog_in, dskip_in, gate_in,
+           hid, win, wdt, wdt_f, wout, ures, h, pre, act, v, g, dtp, state, pbuf, sib, far, near, comb, stats, nw, cw, gw, hp,
+           wsem, hsem, psem, ssend, srecv, msend, mrecv):
     n_layers, n_steps, d_model = ures.shape
     width = v.shape[1]
     conv_ch = act.shape[1]
@@ -44,6 +46,7 @@
     n_chunks = n_steps // CHUNK
     n_tasks = n_layers * n_chunks
     n_chips = tp_size // 2
+    n_tiles = pre.shape[1] // TILE
     half_rows = CHUNK // 2
     slice_rows = half_rows // n_chips
     piece = slice_rows // 2
@@ -68,26 +71,42 @@
         return pltpu.make_async_copy(hid_hbm.at[rows], hid.at[rows], hsem.at[i])
 
     def load_in(layer):
-        return (
-            pltpu.make_async_copy(wz_hbm.at[layer], win.at[layer, :, pl.ds(0, width)], wsem.at[layer, 0]),
-            pltpu.make_async_copy(wx_hbm.at[layer], win.at[layer, :, pl.ds(width, width)], wsem.at[layer, 1]),
-            pltpu.make_async_copy(wbc_hbm.at[layer], win.at[layer, :, pl.ds(2 * width, 2 * n_state)], wsem.at[layer, 2]),
-            pltpu.make_async_copy(wdt_hbm.at[layer], wdt.at[layer], wsem.at[layer, 3]),
-        )
+        copies = []
+        for w_hbm, first, n_cols in ((wz_hbm, 0, width), (wx_hbm, width, width), (wbc_hbm, 2 * width, 2 * n_state)):
+            done = 0
+            while done < n_cols:
+                n = min(TILE - (first + done) % TILE, n_cols - done)
+                at = first + done
+                copies.append(pltpu.make_async_copy(w_hbm.at[layer, :, pl.ds(done, n)], win.at[layer, :, pl.ds(at, n)],
+                                                    wsem.at[layer, at // TILE]))
+                done += n
+        return copies
+
+    def wait_in(layer, tile):
+        ref = win.at[layer, :, pl.ds(pl.multiple_of(tile * TILE, TILE), TILE)]
+        pltpu.make_async_copy(ref, ref, wsem.at[layer, tile]).wait()
 
     def load_out(layer):
-        return pltpu.make_async_copy(wout_hbm.at[layer], wout.at[layer], wsem.at[layer, 4])
-
+        return pltpu.make_async_copy(wout_hbm.at[layer], wout.at[layer], wsem.at[layer, n_tiles])
+
+    params = ((norm_hbm, norm_in), (wdt_hbm, wdt_in), (convx_hbm, convx_in), (convbc_hbm, convbc_in), (biasx_hbm, biasx_in),
+              (biasbc_hbm, biasbc_in), (dtb_hbm, dtb_in), (alog_hbm, alog_in), (dskip_hbm, dskip_in), (gate_hbm, gate_in))
+    small = [pltpu.make_async_copy(src, dst, psem.at[i]) for i, (src, dst) in enumerate(params)]
     load_hid(0).start()
-    for layer in range(n_layers):
-        for cp in load_in(layer):
-            cp.start()
-        load_out(layer).start()
-        if layer == 0:
-            for i in range(1, n_chunks):
-                load_hid(i).start()
+    for cp in small:
+        cp.start()
+    for cp in load_in(0):
+        cp.start()
+    for cp in small:
+        cp.wait()
 
     hp[...] = jnp.zeros_like(hp)
+    wdt_f[...] = jnp.zeros_like(wdt_f)
+    for n in range(n_heads):
+        cols = wdt_in[n].astype(F32)
+        for layer in range(n_layers):
+            wdt_f[layer, n:n + 1, :] = cols[layer:layer + 1, :]
+    wdt[...] = wdt_f[...].astype(BF16)
     dtp[...] = jnp.zeros_like(dtp)
     for layer in range(n_layers):
         nw[layer, 0:1, :] = norm_in[layer:layer + 1, :].astype(F32)
@@ -191,8 +210,6 @@
 
         @pl.when(row0 == 0)
         def _():
-            for cp in load_in(layer):
-                cp.wait()
             pre[0:HALO, :] = jnp.zeros((HALO, pre.shape[1]), F32)
 
         @pl.when(row0 > 0)
@@ -217,13 +234,31 @@
             norm(lambda r: ures[jnp.maximum(layer - 1, 0), pl.ds(r, 16), :])
 
         def tile(i, carry):
-            o = pl.multiple_of(i * 256, 256)
-            prod = jnp.dot(h[...], win[layer, :, pl.ds(o, 256)], preferred_element_type=F32)
-            pre[HALO:HALO + CHUNK, pl.ds(o, 256)] = prod.astype(BF16).astype(F32)
+            @pl.when(row0 == 0)
+            def _():
+                wait_in(layer, i)
+            o = pl.multiple_of(i * TILE, TILE)
+            prod = jnp.dot(h[...], win[layer, :, pl.ds(o, TILE)], preferred_element_type=F32)
+            pre[HALO:HALO + CHUNK, pl.ds(o, TILE)] = prod.astype(BF16).astype(F32)
             return carry
-        lax.fori_loop(0, pre.shape[1] // 256, tile, 0)
-        prod = jnp.dot(h[...], wdt[layer], preferred_element_type=F32)
-        dtp[:, 0:n_heads] = prod.astype(BF16).astype(F32)
+        lax.fori_loop(0, pre.shape[1] // TILE, tile, 0)
+        prod = lax.dot_general(h[...], wdt[layer], (((1,), (1,)), ((), ())), preferred_element_type=F32)
+        dtp[:, 0:wdt.shape[1]] = prod.astype(BF16).astype(F32)
+
+        @pl.when(t == 0)
+        def _():
+            load_out(0).start()
+            for i in range(1, n_chunks):
+                load_hid(i).start()
+
+        @pl.when((row0 == CHUNK) & (layer < n_layers - 1))
+        def _():
+            for k in range(1, n_layers):
+                @pl.when(layer == k - 1)
+                def _():
+                    for cp in load_in(k):
+                        cp.start()
+                    load_out(k).start()
 
     def mix(t):
         slot = lax.rem(t, SLOTS)
@@ -315,10 +350,10 @@
         buf = pbuf.at[lax.rem(t, 2)]
 
         def tile(i, carry):
-            o = pl.multiple_of(i * 256, 256)
-            buf[:, pl.ds(o, 256)] = jnp.dot(g[...], wout[layer, :, pl.ds(o, 256)], preferred_element_type=F32)
+            o = pl.multiple_of(i * TILE, TILE)
+            buf[:, pl.ds(o, TILE)] = jnp.dot(g[...], wout[layer, :, pl.ds(o, TILE)], preferred_element_type=F32)
             return carry
-        lax.fori_loop(0, d_model // 256, tile, 0)
+        lax.fori_loop(0, d_model // TILE, tile, 0)
         msg_rs(t, SIB).start()
 
     def pair_sum(t):
@@ -389,18 +424,11 @@
 
         @pl.when(layer == n_layers - 1)
         def _():
-            rows = pl.ds(row0, CHUNK)
-
             def block(i, carry):
-                r = pl.multiple_of(i * 16, 16)
-                ost[pl.ds(r, 16), :] = ures[layer, pl.ds(pl.multiple_of(row0 + r, 16), 16), :].astype(BF16)
+                rows = pl.ds(pl.multiple_of(row0 + i * 16, 16), 16)
+                out[rows, :] = ures[layer, rows, :].astype(BF16)
                 return carry
-
-            @pl.when(row0 > 0)
-            def _():
-                pltpu.make_async_copy(ost, out_hbm.at[rows], osem).wait()
             lax.fori_loop(0, CHUNK // 16, block, 0)
-            pltpu.make_async_copy(ost, out_hbm.at[rows], osem).start()
 
     def guarded(step, t):
         @pl.when((t >= 0) & (t < n_tasks))
@@ -409,36 +437,36 @@
 
     def iteration(t, carry):
         guarded(mix, t)
-        guarded(forward, t - 3)
         guarded(pair_sum, t - 1)
         guarded(finish, t - 2)
         guarded(in_proj, t + 1)
+        guarded(out_proj, t)
         guarded(relay_sum, t - 1)
-        guarded(out_proj, t)
+        guarded(forward, t - 3)
         guarded(collect, t - 4)
         return carry
     lax.fori_loop(-1, n_tasks + 4, iteration, 0)
-    pltpu.make_async_copy(ost, out_hbm.at[pl.ds(0, CHUNK)], osem).wait()
 
 
 def layers(tp_size, hidden, norm_w, w_z, w_x, w_bc, w_dt, conv_x, conv_bc, bias_x, bias_bc, dt_bias, a_log, d_skip, gate_w, w_out):
     n_batch, n_steps, d_model = hidden.shape
     n_layers, conv_width, width = conv_x.shape
-    n_heads = dt_bias.shape[-1]
+    head_rows = pl.cdiv(dt_bias.shape[-1], 16) * 16
+    w_dt = jnp.transpose(w_dt, (2, 0, 1))
     state2 = w_bc.shape[-1]
     piece = CHUNK // tp_size // 2
     any_spec = pl.BlockSpec(memory_space=pl.ANY)
-    vmem_spec = pl.BlockSpec(memory_space=pltpu.VMEM)
     dma = pltpu.SemaphoreType.DMA
     run = pl.pallas_call(
         functools.partial(kernel, tp_size, conv_width),
-        out_shape=jax.ShapeDtypeStruct((n_steps, d_model), BF16),
-        in_specs=[any_spec, vmem_spec, any_spec, any_spec, any_spec, any_spec] + [vmem_spec] * 8 + [any_spec],
-        out_specs=any_spec,
-        scratch_shapes=[
+        out_shape=pltpu.VMEM((n_steps, d_model), BF16),
+        in_specs=[any_spec] * 15,
+        out_specs=pl.BlockSpec(memory_space=pltpu.VMEM),
+        scratch_shapes=[pltpu.VMEM(p.shape, p.dtype) for p in (norm_w, w_dt, conv_x, conv_bc, bias_x, bias_bc, dt_bias, a_log, d_skip, gate_w)] + [
             pltpu.VMEM((n_steps, d_model), BF16),
             pltpu.VMEM((n_layers, d_model, 2 * width + state2), BF16),
-            pltpu.VMEM((n_layers, d_model, n_heads), BF16),
+            pltpu.VMEM((n_layers, head_rows, d_model), BF16),
+            pltpu.VMEM((n_layers, head_rows, d_model), F32),
             pltpu.VMEM((n_layers, width, d_model), BF16),
             pltpu.VMEM((n_layers, n_steps, d_model), F32),
             pltpu.VMEM((CHUNK, d_model), BF16),
@@ -458,11 +486,10 @@
             pltpu.VMEM((n_layers, 8, width + state2), F32),
             pltpu.VMEM((n_layers, 8, width), F32),
             pltpu.VMEM((n_layers, 8, LANES), F32),
-            pltpu.VMEM((CHUNK, d_model), BF16),
-            dma((n_layers, 5)), dma((n_steps // CHUNK,)), dma,
+            dma((n_layers, (2 * width + state2) // TILE + 1)), dma((n_steps // CHUNK,)), dma((10,)),
             dma((SLOTS, tp_size)), dma((SLOTS, tp_size)), dma((SLOTS, 15)), dma((SLOTS, 15)),
         ],
-        compiler_params=pltpu.CompilerParams(collective_id=0, has_side_effects=True, vmem_limit_bytes=67_043_328),
+        compiler_params=pltpu.CompilerParams(collective_id=0, has_side_effects=True, vmem_limit_bytes=62_000_000),
     )
     outs = [run(hidden[i], norm_w, w_z, w_x, w_bc, w_dt, conv_x, conv_bc, bias_x, bias_bc, dt_bias, a_log, d_skip, gate_w, w_out)
             for i in range(n_batch)]

time: 193 us -> 168 us (0.87)
  Pallas kernels: 187 us -> 166 us
  local copies, waits for them, and re-layouts: 6.53 us -> 1.93 us
    pallas_call x1, Pallas kernels: 187 us -> 166 us  [layers(): run(hidden[i], norm_w, w_z, w_x, w_bc, w_dt, conv_x, conv_bc, bias_x, bia...]
    unnamed x2 -> x1, local copies, waits for them, and re-layouts: 6.53 us -> 1.93 us
where the time goes in v2:
time: 168 us
  Pallas kernels  166 us (99%)
  local copies, waits for them, and re-layouts  1.93 us (1%)
    pallas_call x1, Pallas kernels, layers(): run(hidden[i], norm_w, w_z, w_x, w_bc, w_dt, conv_x, conv_bc, bias_x, bia...  166 us

profile of v2, /device:TPU:81, one launch (start us, length us, event | category | flops | bytes accessed | tf_op | source)
XLA Modules:
  0.0 168.3 jit_solution(1029995771719274348)
XLA Ops:
  0.0 166.3 %shard_map.145 = bf16[768,2560]{1,0:T(8,128)(2,1)S(1)} custom-call(bf16[768,2560]{1,0:T(8,128)(2,1)} %bitcast.4, bf16[2,2560]{1,0:T(2,128)(2,1)} %norm_hbm.1, bf16[2,2560,640]{2,1,0:T(8,128)(2,1)} %wz_hbm.1, bf16[2,2560,640]{2,1,0:T(8,128)(2,1)} %wx_hbm.1, bf16[2,2560,256]{2,1,0:T(8,128)(2,1)} %wbc_hbm.1, bf16[10,2,2560]{2,1,0:T(2,128)(2,1)} %bitcast.5, ...), custom_call_target="tpu_custom_call" | custom-call | tf_op jit(solution)/shard_map/pallas_call | solution.py:494
  166.3 1.9 %copy.17 = bf16[1,768,2560]{2,1,0:T(8,128)(2,1)} copy(bf16[1,768,2560]{2,1,0:T(8,128)(2,1)S(1)} %bitcast.3) | data formatting | bytes 7864320

commit v3 on v2

--- a/solution.py
+++ b/solution.py
@@ -15,9 +15,10 @@
 LANES = 128
 CHUNK = 128
 SLOTS = 4
+SEM_SLOTS = 6
 HALO = 8
 TILE = 256
-SIB, FAR_P, FAR_M, NEAR_P, NEAR_M, COMB_P, COMB_M, AG_P, AG_M, FW_P, FW_M, D0, D1, D2, D3 = range(15)
+(SIB, FAR_P, FAR_M, NEAR_P, NEAR_M, COMB_P, COMB_M, OWN_P1, OWN_P2, OWN_M1, OWN_M2, FW_P, FW_M, D0, D1, D2, D3) = range(17)
 
 
 def full_dot(a, b, dims=(((1,), (0,)), ((), ()))):
@@ -125,7 +126,8 @@
         layer = t // n_chunks
         return layer, pl.multiple_of((t - layer * n_chunks) * CHUNK, CHUNK)
 
-    def remote(src, dst, slot, kind, dev):
+    def remote(src, dst, t, kind, dev):
+        slot = lax.rem(t, SEM_SLOTS)
         return pltpu.make_async_remote_copy(src_ref=src, dst_ref=dst, send_sem=msend.at[slot, kind], recv_sem=mrecv.at[slot, kind],
                                             device_id=dev, device_id_type=MESH)
 
@@ -140,61 +142,41 @@
             return buf.at[pl.ds(pl.multiple_of(slice_at(core, j) + part * piece, piece), piece)]
         if kind == SIB:
             other = pl.multiple_of((1 - core) * half_rows, half_rows)
-            return remote(buf.at[pl.ds(other, half_rows)], sib.at[lax.rem(t, 2)], slot, kind, dev_sib)
+            return remote(buf.at[pl.ds(other, half_rows)], sib.at[lax.rem(t, 2)], t, kind, dev_sib)
         if kind == FAR_P:
-            return remote(src(opp, 1), far.at[slot, 0], slot, kind, dev_nxt)
+            return remote(src(opp, 1), far.at[slot, 0], t, kind, dev_nxt)
         if kind == FAR_M:
-            return remote(src(opp, 0), far.at[slot, 1], slot, kind, dev_prv)
+            return remote(src(opp, 0), far.at[slot, 1], t, kind, dev_prv)
         if kind == NEAR_P:
-            return remote(src(nxt, 0), near.at[slot, 0], slot, kind, dev_nxt)
+            return remote(src(nxt, 0), near.at[slot, 0], t, kind, dev_nxt)
         if kind == NEAR_M:
-            return remote(src(prv, 1), near.at[slot, 1], slot, kind, dev_prv)
+            return remote(src(prv, 1), near.at[slot, 1], t, kind, dev_prv)
         if kind == COMB_P:
-            return remote(src(nxt, 1), comb.at[slot, 0], slot, kind, dev_nxt)
-        return remote(src(prv, 0), comb.at[slot, 1], slot, kind, dev_prv)
-
-    def msg_ag(t, kind, c=None):
-        slot = lax.rem(t, SLOTS)
-        layer, row0 = where_of(t)
-        c = core if c is None else c
-
-        def rows(j, part=None):
-            base = row0 + slice_at(c, j)
-            if part is None:
-                return ures.at[layer, pl.ds(pl.multiple_of(base, slice_rows), slice_rows)]
-            return ures.at[layer, pl.ds(pl.multiple_of(base + part * piece, piece), piece)]
-        ref, dev = {
-            AG_P: lambda: (rows(chip), dev_nxt),
-            AG_M: lambda: (rows(chip), dev_prv),
-            FW_P: lambda: (rows(prv, 0), dev_nxt),
-            FW_M: lambda: (rows(nxt, 1), dev_prv),
-            D0: lambda: (rows(chip), dev_sib),
-            D1: lambda: (rows(prv), dev_sib),
-            D2: lambda: (rows(nxt), dev_sib),
-            D3: lambda: (rows(opp), dev_sib),
-        }[kind]()
-        return remote(ref, ref, slot, kind, dev)
+            return remote(src(nxt, 1), comb.at[slot, 0], t, kind, dev_nxt)
+        return remote(src(prv, 0), comb.at[slot, 1], t, kind, dev_prv)
+
+    def ag_rows(t, c, j, part=None):
+        layer, row0 = where_of(t)
+        base = row0 + slice_at(c, j)
+        if part is None:
+            return ures.at[layer, pl.ds(pl.multiple_of(base, slice_rows), slice_rows)]
+        return ures.at[layer, pl.ds(pl.multiple_of(base + part * piece, piece), piece)]
+
+    ag_sent = {OWN_P1: (chip, 0, dev_nxt), OWN_P2: (chip, 1, dev_nxt), OWN_M1: (chip, 1, dev_prv), OWN_M2: (chip, 0, dev_prv),
+               FW_P: (prv, 0, dev_nxt), FW_M: (nxt, 1, dev_prv),
+               D0: (chip, None, dev_sib), D1: (prv, None, dev_sib), D2: (nxt, None, dev_sib), D3: (opp, None, dev_sib)}
+    ag_got = {OWN_P1: (core, prv, 0), OWN_P2: (core, prv, 1), OWN_M1: (core, nxt, 1), OWN_M2: (core, nxt, 0),
+              FW_P: (core, opp, 0), FW_M: (core, opp, 1),
+              D0: (1 - core, chip, None), D1: (1 - core, prv, None), D2: (1 - core, nxt, None), D3: (1 - core, opp, None)}
+
+    def msg_ag(t, kind):
+        j, part, dev = ag_sent[kind]
+        ref = ag_rows(t, core, j, part)
+        return remote(ref, ref, t, kind, dev)
 
     def wait_ag(t, kind):
-        slot = lax.rem(t, SLOTS)
-        layer, row0 = where_of(t)
-
-        def rows(c, j, part=None):
-            base = row0 + slice_at(c, j)
-            if part is None:
-                return ures.at[layer, pl.ds(pl.multiple_of(base, slice_rows), slice_rows)]
-            return ures.at[layer, pl.ds(pl.multiple_of(base + part * piece, piece), piece)]
-        ref = {
-            AG_P: lambda: rows(core, prv),
-            AG_M: lambda: rows(core, nxt),
-            FW_P: lambda: rows(core, opp, 0),
-            FW_M: lambda: rows(core, opp, 1),
-            D0: lambda: rows(1 - core, chip),
-            D1: lambda: rows(1 - core, prv),
-            D2: lambda: rows(1 - core, nxt),
-            D3: lambda: rows(1 - core, opp),
-        }[kind]()
-        remote(ref, ref, slot, kind, dev_sib).wait_recv()
+        ref = ag_rows(t, *ag_got[kind])
+        remote(ref, ref, t, kind, dev_sib).wait_recv()
 
     def msg_stat(t, off):
         slot = lax.rem(t, SLOTS)
@@ -399,27 +381,27 @@
         @pl.when(layer > 0)
         def _():
             store(ures[jnp.maximum(layer - 1, 0), dst, :])
-        for kind in (AG_P, AG_M, D0):
+        for kind in (OWN_P1, OWN_M1, OWN_P2, OWN_M2, D0):
             msg_ag(t, kind).start()
         for kind in (SIB, FAR_P, FAR_M, NEAR_P, NEAR_M, COMB_P, COMB_M):
             msg_rs(t, kind).wait_send()
 
     def forward(t):
-        wait_ag(t, AG_P)
-        msg_ag(t, FW_P).start()
-        wait_ag(t, AG_M)
-        msg_ag(t, FW_M).start()
-        msg_ag(t, D1).start()
-        msg_ag(t, D2).start()
+        for wait, send in ((OWN_P1, FW_P), (OWN_M1, FW_M)):
+            wait_ag(t, wait)
+            msg_ag(t, send).start()
+
+    def share(t):
+        for waits, send in (((OWN_P2,), D1), ((OWN_M2,), D2), ((FW_P, FW_M), D3)):
+            for kind in waits:
+                wait_ag(t, kind)
+            msg_ag(t, send).start()
 
     def collect(t):
         layer, row0 = where_of(t)
-        wait_ag(t, FW_P)
-        wait_ag(t, FW_M)
-        msg_ag(t, D3).start()
         for kind in (D0, D1, D2, D3):
             wait_ag(t, kind)
-        for kind in (AG_P, AG_M, FW_P, FW_M, D0, D1, D2, D3):
+        for kind in ag_sent:
             msg_ag(t, kind).wait_send()
 
         @pl.when(layer == n_layers - 1)
@@ -437,15 +419,16 @@
 
     def iteration(t, carry):
         guarded(mix, t)
+        guarded(collect, t - 5)
         guarded(pair_sum, t - 1)
+        guarded(in_proj, t + 1)
         guarded(finish, t - 2)
-        guarded(in_proj, t + 1)
         guarded(out_proj, t)
         guarded(relay_sum, t - 1)
         guarded(forward, t - 3)
-        guarded(collect, t - 4)
+        guarded(share, t - 4)
         return carry
-    lax.fori_loop(-1, n_tasks + 4, iteration, 0)
+    lax.fori_loop(-1, n_tasks + 5, iteration, 0)
 
 
 def layers(tp_size, hidden, norm_w, w_z, w_x, w_bc, w_dt, conv_x, conv_bc, bias_x, bias_bc, dt_bias, a_log, d_skip, gate_w, w_out):
@@ -487,7 +470,7 @@
             pltpu.VMEM((n_layers, 8, width), F32),
             pltpu.VMEM((n_layers, 8, LANES), F32),
             dma((n_layers, (2 * width + state2) // TILE + 1)), dma((n_steps // CHUNK,)), dma((10,)),
-            dma((SLOTS, tp_size)), dma((SLOTS, tp_size)), dma((SLOTS, 15)), dma((SLOTS, 15)),
+            dma((SLOTS, tp_size)), dma((SLOTS, tp_size)), dma((SEM_SLOTS, 17)), dma((SEM_SLOTS, 17)),
         ],
         compiler_params=pltpu.CompilerParams(collective_id=0, has_side_effects=True, vmem_limit_bytes=62_000_000),
     )

time: 168 us -> 163 us (0.970)
  Pallas kernels: 166 us -> 161 us
    pallas_call x1, Pallas kernels: 166 us -> 161 us  [layers(): run(hidden[i], norm_w, w_z, w_x, w_bc, w_dt, conv_x, conv_bc, bias_x, bia...]
where the time goes in v3:
time: 163 us
  Pallas kernels  161 us (99%)
  local copies, waits for them, and re-layouts  1.93 us (1%)
    pallas_call x1, Pallas kernels, layers(): run(hidden[i], norm_w, w_z, w_x, w_bc, w_dt, conv_x, conv_bc, bias_x, bia...  161 us

profile of v3, /device:TPU:81, one launch (start us, length us, event | category | flops | bytes accessed | tf_op | source)
XLA Modules:
  0.0 163.2 jit_solution(7208328629621240643)
XLA Ops:
  0.0 161.2 %shard_map.145 = bf16[768,2560]{1,0:T(8,128)(2,1)S(1)} custom-call(bf16[768,2560]{1,0:T(8,128)(2,1)} %bitcast.4, bf16[2,2560]{1,0:T(2,128)(2,1)} %norm_hbm.1, bf16[2,2560,640]{2,1,0:T(8,128)(2,1)} %wz_hbm.1, bf16[2,2560,640]{2,1,0:T(8,128)(2,1)} %wx_hbm.1, bf16[2,2560,256]{2,1,0:T(8,128)(2,1)} %wbc_hbm.1, bf16[10,2,2560]{2,1,0:T(2,128)(2,1)} %bitcast.5, ...), custom_call_target="tpu_custom_call" | custom-call | tf_op jit(solution)/shard_map/pallas_call | solution.py:477
  161.2 1.9 %copy.17 = bf16[1,768,2560]{2,1,0:T(8,128)(2,1)} copy(bf16[1,768,2560]{2,1,0:T(8,128)(2,1)S(1)} %bitcast.3) | data formatting | bytes 7864320

commit v4 on v3

--- a/solution.py
+++ b/solution.py
@@ -10,7 +10,6 @@
 EPSILON = 1e-5
 F32 = jnp.float32
 BF16 = jnp.bfloat16
-FULL = lax.Precision.HIGHEST
 MESH = pl.DeviceIdType.MESH
 LANES = 128
 CHUNK = 128
@@ -21,8 +20,26 @@
 (SIB, FAR_P, FAR_M, NEAR_P, NEAR_M, COMB_P, COMB_M, OWN_P1, OWN_P2, OWN_M1, OWN_M2, FW_P, FW_M, D0, D1, D2, D3) = range(17)
 
 
-def full_dot(a, b, dims=(((1,), (0,)), ((), ()))):
-    return lax.dot_general(a, b, dims, precision=FULL, preferred_element_type=F32)
+def fast_dot(a, b, dims=(((1,), (0,)), ((), ()))):
+    return lax.dot_general(a, b, dims, preferred_element_type=F32)
+
+
+def split(m):
+    hi = m.astype(BF16)
+    rest = m - hi.astype(F32)
+    mid = rest.astype(BF16)
+    return hi, mid, (rest - mid.astype(F32)).astype(BF16)
+
+
+def left_parts(m):
+    hi, mid, lo = split(m)
+    return jnp.concatenate([hi, hi], axis=1), jnp.concatenate([mid, mid], axis=1), jnp.concatenate([lo, hi], axis=1)
+
+
+def three_dots(p1, p2, p3, parts, cols):
+    n = parts.shape[0] // 3
+    upper = parts[0:2 * n, cols]
+    return (fast_dot(p3, parts[n:3 * n, cols]) + fast_dot(p2, upper)) + fast_dot(p1, upper)
 
 
 def silu(a):
@@ -36,7 +53,7 @@
 def kernel(tp_size, conv_width, hid_hbm, norm_hbm, wz_hbm, wx_hbm, wbc_hbm, wdt_hbm, convx_hbm, convbc_hbm, biasx_hbm, biasbc_hbm,
            dtb_hbm, alog_hbm, dskip_hbm, gate_hbm, wout_hbm, out,
            norm_in, wdt_in, convx_in, convbc_in, biasx_in, biasbc_in, dtb_in, alog_in, dskip_in, gate_in,
-           hid, win, wdt, wdt_f, wout, ures, h, pre, act, v, g, dtp, state, pbuf, sib, far, near, comb, stats, nw, cw, gw, hp,
+           hid, win, wdt, wdt_f, wout, ures, h, pre, act, v, g, dtp, state, state3, weighted3, pbuf, sib, far, near, comb, stats, nw, cw, gw, hp,
            wsem, hsem, psem, ssend, srecv, msend, mrecv):
     n_layers, n_steps, d_model = ures.shape
     width = v.shape[1]
@@ -249,6 +266,7 @@
         @pl.when(row0 == 0)
         def _():
             state[...] = jnp.zeros_like(state)
+            state3[...] = jnp.zeros_like(state3)
 
         def conv(i, carry):
             o = pl.multiple_of(i * LANES, LANES)
@@ -267,7 +285,8 @@
         left_row = left[0:1, :]
         dt = softplus(dtp[...] + hp[layer, 0:1, :])
         a = -dt * jnp.exp(hp[layer, 1:2, :])
-        a_cum = full_dot(jnp.where(lower, 1.0, 0.0).astype(F32), a)
+        ones = jnp.where(lower, 1.0, 0.0).astype(BF16)
+        a_cum = sum(fast_dot(ones, part) for part in reversed(split(a)))
         a_cum_t = a_cum.T
         a_last = a_cum[CHUNK - 1:CHUNK, :]
         from_start = jnp.exp(a_cum)
@@ -275,9 +294,16 @@
         whole = jnp.exp(a_last)
         skip = hp[layer, 2:3, :]
         b = act[:, width:width + n_state]
-        c = act[:, width + n_state:conv_ch]
-        c_dot_b = full_dot(c, b, (((1,), (1,)), ((), ())))
-        b_t = b.T
+        c1, c2, c3 = left_parts(act[:, width + n_state:conv_ch])
+        bh, bm, bl = split(b)
+        nt = (((1,), (1,)), ((), ()))
+        b_mh = jnp.concatenate([bm, bh], axis=1)
+        c_dot_b = (fast_dot(c3, jnp.concatenate([bh, bl], axis=1), nt) + fast_dot(c2, b_mh, nt)) + fast_dot(c1, b_mh, nt)
+        c_dot_b = jnp.where(lower, c_dot_b, 0.0)
+        b1, b2, b3 = left_parts(b.T)
+        for o in range(0, width, TILE):
+            cols = slice(o, min(o + TILE, width))
+            v[:, cols] = three_dots(c1, c2, c3, state3, cols)
         sq = jnp.zeros((CHUNK, LANES), F32)
         for p in range(width // LANES):
             cols = slice(p * LANES, (p + 1) * LANES)
@@ -291,14 +317,19 @@
 
             def mixer(n):
                 seg = a_cum[:, n:n + 1] - a_cum_t[n:n + 1, :]
-                return jnp.where(lower, jnp.exp(jnp.minimum(seg, 0.0)), 0.0) * c_dot_b
+                return split(jnp.exp(jnp.minimum(seg, 0.0)) * c_dot_b)
             x = act[:, cols]
             x_dt = x * spread(dt)
-            both = jnp.concatenate([jnp.where(left, x_dt, 0.0), jnp.where(left, 0.0, x_dt)], axis=0)
-            y = full_dot(jnp.concatenate([mixer(h0), mixer(h1)], axis=1), both)
-            s_in = state[:, cols]
-            y = y + full_dot(c, s_in) * spread(from_start)
-            state[:, cols] = s_in * spread_row(whole) + full_dot(b_t, x_dt * spread(to_end))
+            wh, wm, wl = split(x_dt * spread(to_end))
+            weighted3[0:CHUNK, cols] = wm
+            weighted3[CHUNK:2 * CHUNK, cols] = wh
+            weighted3[2 * CHUNK:3 * CHUNK, cols] = wl
+            xh, xm, xl = split(jnp.concatenate([jnp.where(left, x_dt, 0.0), jnp.where(left, 0.0, x_dt)], axis=0))
+            mh, mm, ml = (jnp.concatenate(pair, axis=1) for pair in zip(mixer(h0), mixer(h1)))
+            x_hm = jnp.concatenate([xh, xm], axis=1)
+            wide = fast_dot(mm, x_hm) + fast_dot(mh, x_hm)
+            y = (fast_dot(ml, xh) + fast_dot(mh, xl)) + wide[:, LANES:] + wide[:, :LANES]
+            y = y + v[:, cols] * spread(from_start)
             y = y + spread_row(skip) * x
             gated = y * silu(pre[HALO:HALO + CHUNK, cols])
             v[:, cols] = gated
@@ -307,6 +338,16 @@
         stats[slot, me] = jnp.broadcast_to(total, (8, CHUNK))
         for off in range(1, tp_size):
             msg_stat(t, off).start()
+        for o in range(0, width, TILE):
+            cols = slice(o, min(o + TILE, width))
+            decay = jnp.concatenate([jnp.where(left_row, whole[:, n:n + 1], whole[:, n + 1:n + 2])
+                                     for n in range(o // head_dim, cols.stop // head_dim, 2)], axis=1)
+            s_new = state[:, cols] * decay + three_dots(b1, b2, b3, weighted3, cols)
+            state[:, cols] = s_new
+            sh, sm, sl = split(s_new)
+            state3[0:n_state, cols] = sm
+            state3[n_state:2 * n_state, cols] = sh
+            state3[2 * n_state:3 * n_state, cols] = sl
 
     def out_proj(t):
         slot = lax.rem(t, SLOTS)
@@ -459,6 +500,8 @@
             pltpu.VMEM((CHUNK, width), BF16),
             pltpu.VMEM((CHUNK, LANES), F32),
             pltpu.VMEM((state2 // 2, width), F32),
+            pltpu.VMEM((3 * state2 // 2, width), BF16),
+            pltpu.VMEM((3 * CHUNK, width), BF16),
             pltpu.VMEM((2, CHUNK, d_model), F32),
             pltpu.VMEM((2, CHUNK // 2, d_model), F32),
             pltpu.VMEM((SLOTS, 2, piece, d_model), F32),

time: 163 us -> 162 us (level)
  no operation moved by 1% of the time
where the time goes in v4:
time: 162 us
  Pallas kernels  160 us (99%)
  local copies, waits for them, and re-layouts  1.93 us (1%)
    pallas_call x1, Pallas kernels, layers(): run(hidden[i], norm_w, w_z, w_x, w_bc, w_dt, conv_x, conv_bc, bias_x, bia...  160 us

profile of v4, /device:TPU:81, one launch (start us, length us, event | category | flops | bytes accessed | tf_op | source)
XLA Modules:
  0.0 162.3 jit_solution(15308802326818660880)
XLA Ops:
  0.0 160.4 %shard_map.145 = bf16[768,2560]{1,0:T(8,128)(2,1)S(1)} custom-call(bf16[768,2560]{1,0:T(8,128)(2,1)} %bitcast.4, bf16[2,2560]{1,0:T(2,128)(2,1)} %norm_hbm.1, bf16[2,2560,640]{2,1,0:T(8,128)(2,1)} %wz_hbm.1, bf16[2,2560,640]{2,1,0:T(8,128)(2,1)} %wx_hbm.1, bf16[2,2560,256]{2,1,0:T(8,128)(2,1)} %wbc_hbm.1, bf16[10,2,2560]{2,1,0:T(2,128)(2,1)} %bitcast.5, ...), custom_call_target="tpu_custom_call" | custom-call | tf_op jit(solution)/shard_map/pallas_call | solution.py:520
  160.4 1.9 %copy.17 = bf16[1,768,2560]{2,1,0:T(8,128)(2,1)} copy(bf16[1,768,2560]{2,1,0:T(8,128)(2,1)S(1)} %bitcast.3) | data formatting | bytes 7864320

commit v5 on v4

--- a/solution.py
+++ b/solution.py
@@ -115,27 +115,30 @@
         cp.start()
     for cp in load_in(0):
         cp.start()
-    for cp in small:
-        cp.wait()
-
-    hp[...] = jnp.zeros_like(hp)
-    wdt_f[...] = jnp.zeros_like(wdt_f)
-    for n in range(n_heads):
-        cols = wdt_in[n].astype(F32)
-        for layer in range(n_layers):
-            wdt_f[layer, n:n + 1, :] = cols[layer:layer + 1, :]
-    wdt[...] = wdt_f[...].astype(BF16)
-    dtp[...] = jnp.zeros_like(dtp)
+    small[0].wait()
     for layer in range(n_layers):
         nw[layer, 0:1, :] = norm_in[layer:layer + 1, :].astype(F32)
-        gw[layer, 0:1, :] = gate_in[layer:layer + 1, :].astype(F32)
-        cw[layer, 0:conv_width, 0:width] = convx_in[layer].astype(F32)
-        cw[layer, 0:conv_width, width:conv_ch] = convbc_in[layer].astype(F32)
-        cw[layer, conv_width:conv_width + 1, 0:width] = biasx_in[layer:layer + 1, :].astype(F32)
-        cw[layer, conv_width:conv_width + 1, width:conv_ch] = biasbc_in[layer:layer + 1, :].astype(F32)
-        hp[layer, 0:1, 0:n_heads] = dtb_in[layer:layer + 1, :]
-        hp[layer, 1:2, 0:n_heads] = alog_in[layer:layer + 1, :]
-        hp[layer, 2:3, 0:n_heads] = dskip_in[layer:layer + 1, :]
+
+    def widen():
+        for cp in small[1:]:
+            cp.wait()
+        hp[...] = jnp.zeros_like(hp)
+        wdt_f[...] = jnp.zeros_like(wdt_f)
+        for n in range(n_heads):
+            cols = wdt_in[n].astype(F32)
+            for layer in range(n_layers):
+                wdt_f[layer, n:n + 1, :] = cols[layer:layer + 1, :]
+        wdt[...] = wdt_f[...].astype(BF16)
+        dtp[...] = jnp.zeros_like(dtp)
+        for layer in range(n_layers):
+            gw[layer, 0:1, :] = gate_in[layer:layer + 1, :].astype(F32)
+            cw[layer, 0:conv_width, 0:width] = convx_in[layer].astype(F32)
+            cw[layer, 0:conv_width, width:conv_ch] = convbc_in[layer].astype(F32)
+            cw[layer, conv_width:conv_width + 1, 0:width] = biasx_in[layer:layer + 1, :].astype(F32)
+            cw[layer, conv_width:conv_width + 1, width:conv_ch] = biasbc_in[layer:layer + 1, :].astype(F32)
+            hp[layer, 0:1, 0:n_heads] = dtb_in[layer:layer + 1, :]
+            hp[layer, 1:2, 0:n_heads] = alog_in[layer:layer + 1, :]
+            hp[layer, 2:3, 0:n_heads] = dskip_in[layer:layer + 1, :]
 
     pl.semaphore_wait(barrier, tp_size - 1)
 
@@ -217,30 +220,34 @@
 
         def norm(load):
             def block(i, carry):
-                r = pl.multiple_of(i * 16, 16)
-                u = load(pl.multiple_of(row0 + r, 16))
+                r = pl.multiple_of(i * 32, 32)
+                u = load(pl.multiple_of(row0 + r, 32))
                 scale = lax.rsqrt(jnp.mean(u * u, axis=-1, keepdims=True) + EPSILON)
-                h[pl.ds(r, 16), :] = (u * scale * nw[layer, 0:1, :]).astype(BF16)
+                h[pl.ds(r, 32), :] = (u * scale * nw[layer, 0:1, :]).astype(BF16)
                 return carry
-            lax.fori_loop(0, CHUNK // 16, block, 0)
+            lax.fori_loop(0, CHUNK // 32, block, 0)
 
         @pl.when(layer == 0)
         def _():
-            norm(lambda r: hid[pl.ds(r, 16), :].astype(F32))
+            norm(lambda r: hid[pl.ds(r, 32), :].astype(F32))
 
         @pl.when(layer > 0)
         def _():
-            norm(lambda r: ures[jnp.maximum(layer - 1, 0), pl.ds(r, 16), :])
+            norm(lambda r: ures[jnp.maximum(layer - 1, 0), pl.ds(r, 32), :])
+
+        pl.when(t == 0)(widen)
+        wide = 2 * TILE
 
         def tile(i, carry):
             @pl.when(row0 == 0)
             def _():
-                wait_in(layer, i)
-            o = pl.multiple_of(i * TILE, TILE)
-            prod = jnp.dot(h[...], win[layer, :, pl.ds(o, TILE)], preferred_element_type=F32)
-            pre[HALO:HALO + CHUNK, pl.ds(o, TILE)] = prod.astype(BF16).astype(F32)
+                wait_in(layer, 2 * i)
+                wait_in(layer, 2 * i + 1)
+            o = pl.multiple_of(i * wide, wide)
+            prod = jnp.dot(h[...], win[layer, :, pl.ds(o, wide)], preferred_element_type=F32)
+            pre[HALO:HALO + CHUNK, pl.ds(o, wide)] = prod.astype(BF16).astype(F32)
             return carry
-        lax.fori_loop(0, pre.shape[1] // TILE, tile, 0)
+        lax.fori_loop(0, pre.shape[1] // wide, tile, 0)
         prod = lax.dot_general(h[...], wdt[layer], (((1,), (1,)), ((), ())), preferred_element_type=F32)
         dtp[:, 0:wdt.shape[1]] = prod.astype(BF16).astype(F32)
 
@@ -376,7 +383,7 @@
             o = pl.multiple_of(i * TILE, TILE)
             buf[:, pl.ds(o, TILE)] = jnp.dot(g[...], wout[layer, :, pl.ds(o, TILE)], preferred_element_type=F32)
             return carry
-        lax.fori_loop(0, d_model // TILE, tile, 0)
+        lax.fori_loop(0, d_model // TILE, tile, 0, unroll=True)
         msg_rs(t, SIB).start()
 
     def pair_sum(t):

time: 162 us -> 158 us (0.975)
  Pallas kernels: 160 us -> 156 us
    pallas_call x1, Pallas kernels: 160 us -> 156 us  [layers(): run(hidden[i], norm_w, w_z, w_x, w_bc, w_dt, conv_x, conv_bc, bias_x, bia...]
where the time goes in v5:
time: 158 us
  Pallas kernels  156 us (99%)
  local copies, waits for them, and re-layouts  1.93 us (1%)
    pallas_call x1, Pallas kernels, layers(): run(hidden[i], norm_w, w_z, w_x, w_bc, w_dt, conv_x, conv_bc, bias_x, bia...  156 us

profile of v5, /device:TPU:81, one launch (start us, length us, event | category | flops | bytes accessed | tf_op | source)
XLA Modules:
  0.0 157.7 jit_solution(15393091925552006163)
XLA Ops:
  0.0 155.7 %shard_map.145 = bf16[768,2560]{1,0:T(8,128)(2,1)S(1)} custom-call(bf16[768,2560]{1,0:T(8,128)(2,1)} %bitcast.4, bf16[2,2560]{1,0:T(2,128)(2,1)} %norm_hbm.1, bf16[2,2560,640]{2,1,0:T(8,128)(2,1)} %wz_hbm.1, bf16[2,2560,640]{2,1,0:T(8,128)(2,1)} %wx_hbm.1, bf16[2,2560,256]{2,1,0:T(8,128)(2,1)} %wbc_hbm.1, bf16[10,2,2560]{2,1,0:T(2,128)(2,1)} %bitcast.5, ...), custom_call_target="tpu_custom_call" | custom-call | tf_op jit(solution)/shard_map/pallas_call | solution.py:527
  155.7 1.9 %copy.17 = bf16[1,768,2560]{2,1,0:T(8,128)(2,1)} copy(bf16[1,768,2560]{2,1,0:T(8,128)(2,1)S(1)} %bitcast.3) | data formatting | bytes 7864320

commit v6 on v5

--- a/solution.py
+++ b/solution.py
@@ -14,7 +14,8 @@
 LANES = 128
 CHUNK = 128
 SLOTS = 4
-SEM_SLOTS = 6
+SEM_SLOTS = 8
+P_SLOTS = 3
 HALO = 8
 TILE = 256
 (SIB, FAR_P, FAR_M, NEAR_P, NEAR_M, COMB_P, COMB_M, OWN_P1, OWN_P2, OWN_M1, OWN_M2, FW_P, FW_M, D0, D1, D2, D3) = range(17)
@@ -143,7 +144,7 @@
     pl.semaphore_wait(barrier, tp_size - 1)
 
     def where_of(t):
-        layer = t // n_chunks
+        layer = sum(jnp.where(t >= k * n_chunks, 1, 0) for k in range(1, n_layers))
         return layer, pl.multiple_of((t - layer * n_chunks) * CHUNK, CHUNK)
 
     def remote(src, dst, t, kind, dev):
@@ -156,7 +157,7 @@
 
     def msg_rs(t, kind):
         slot = lax.rem(t, SLOTS)
-        buf = pbuf.at[lax.rem(t, 2)]
+        buf = pbuf.at[lax.rem(t, P_SLOTS)]
 
         def src(j, part):
             return buf.at[pl.ds(pl.multiple_of(slice_at(core, j) + part * piece, piece), piece)]
@@ -235,7 +236,6 @@
         def _():
             norm(lambda r: ures[jnp.maximum(layer - 1, 0), pl.ds(r, 32), :])
 
-        pl.when(t == 0)(widen)
         wide = 2 * TILE
 
         def tile(i, carry):
@@ -296,8 +296,7 @@
         a_cum = sum(fast_dot(ones, part) for part in reversed(split(a)))
         a_cum_t = a_cum.T
         a_last = a_cum[CHUNK - 1:CHUNK, :]
-        from_start = jnp.exp(a_cum)
-        to_end = jnp.exp(a_last - a_cum)
+        zero = jnp.zeros((CHUNK, LANES), BF16)
         whole = jnp.exp(a_last)
         skip = hp[layer, 2:3, :]
         b = act[:, width:width + n_state]
@@ -322,21 +321,25 @@
             def spread_row(m):
                 return jnp.where(left_row, m[:, h0:h0 + 1], m[:, h1:h1 + 1])
 
-            def mixer(n):
-                seg = a_cum[:, n:n + 1] - a_cum_t[n:n + 1, :]
+            cum0 = jnp.broadcast_to(a_cum[:, h0:h0 + 1], (CHUNK, LANES))
+            cum1 = jnp.broadcast_to(a_cum[:, h1:h1 + 1], (CHUNK, LANES))
+            cum = jnp.where(left, cum0, cum1)
+
+            def mixer(cum_rows, n):
+                seg = cum_rows - a_cum_t[n:n + 1, :]
                 return split(jnp.exp(jnp.minimum(seg, 0.0)) * c_dot_b)
             x = act[:, cols]
             x_dt = x * spread(dt)
-            wh, wm, wl = split(x_dt * spread(to_end))
+            wh, wm, wl = split(x_dt * jnp.exp(spread_row(a_last) - cum))
             weighted3[0:CHUNK, cols] = wm
             weighted3[CHUNK:2 * CHUNK, cols] = wh
             weighted3[2 * CHUNK:3 * CHUNK, cols] = wl
-            xh, xm, xl = split(jnp.concatenate([jnp.where(left, x_dt, 0.0), jnp.where(left, 0.0, x_dt)], axis=0))
-            mh, mm, ml = (jnp.concatenate(pair, axis=1) for pair in zip(mixer(h0), mixer(h1)))
+            xh, xm, xl = (jnp.concatenate([jnp.where(left, part, zero), jnp.where(left, zero, part)], axis=0) for part in split(x_dt))
+            mh, mm, ml = (jnp.concatenate(pair, axis=1) for pair in zip(mixer(cum0, h0), mixer(cum1, h1)))
             x_hm = jnp.concatenate([xh, xm], axis=1)
             wide = fast_dot(mm, x_hm) + fast_dot(mh, x_hm)
             y = (fast_dot(ml, xh) + fast_dot(mh, xl)) + wide[:, LANES:] + wide[:, :LANES]
-            y = y + v[:, cols] * spread(from_start)
+            y = y + v[:, cols] * jnp.exp(cum)
             y = y + spread_row(skip) * x
             gated = y * silu(pre[HALO:HALO + CHUNK, cols])
             v[:, cols] = gated
@@ -377,7 +380,7 @@
         for p in range(width // LANES):
             cols = slice(p * LANES, (p + 1) * LANES)
             g[:, cols] = (v[:, cols] * scale * gw[layer, 0:1, cols]).astype(BF16)
-        buf = pbuf.at[lax.rem(t, 2)]
+        buf = pbuf.at[lax.rem(t, P_SLOTS)]
 
         def tile(i, carry):
             o = pl.multiple_of(i * TILE, TILE)
@@ -388,7 +391,7 @@
 
     def pair_sum(t):
         msg_rs(t, SIB).wait_recv()
-        buf, other = pbuf.at[lax.rem(t, 2)], sib.at[lax.rem(t, 2)]
+        buf, other = pbuf.at[lax.rem(t, P_SLOTS)], sib.at[lax.rem(t, 2)]
 
         def block(i, carry):
             r = pl.multiple_of(i * 8, 8)
@@ -401,7 +404,7 @@
 
     def relay_sum(t):
         slot = lax.rem(t, SLOTS)
-        buf = pbuf.at[lax.rem(t, 2)]
+        buf = pbuf.at[lax.rem(t, P_SLOTS)]
         for way, (wait, send, j, part) in enumerate(((FAR_P, COMB_P, nxt, 1), (FAR_M, COMB_M, prv, 0))):
             msg_rs(t, wait).wait_recv()
             rows = pl.ds(pl.multiple_of(slice_at(core, j) + part * piece, piece), piece)
@@ -411,7 +414,7 @@
     def finish(t):
         slot = lax.rem(t, SLOTS)
         layer, row0 = where_of(t)
-        buf = pbuf.at[lax.rem(t, 2)]
+        buf = pbuf.at[lax.rem(t, P_SLOTS)]
         for kind in (NEAR_P, NEAR_M, COMB_P, COMB_M):
             msg_rs(t, kind).wait_recv()
         base = slice_at(core, chip)
@@ -460,23 +463,29 @@
                 return carry
             lax.fori_loop(0, CHUNK // 16, block, 0)
 
-    def guarded(step, t):
-        @pl.when((t >= 0) & (t < n_tasks))
+    def guarded(step, t, first=0, last=n_tasks):
+        @pl.when((t >= first) & (t < last))
         def _():
             step(t)
 
+    final = n_tasks - n_chunks
+
     def iteration(t, carry):
+        pl.when(t == -1)(widen)
         guarded(mix, t)
-        guarded(collect, t - 5)
         guarded(pair_sum, t - 1)
+        guarded(forward, t - 4)
+        guarded(share, t - 5, last=final)
+        guarded(collect, t - 5, last=final)
         guarded(in_proj, t + 1)
-        guarded(finish, t - 2)
+        guarded(finish, t - 2, last=final)
         guarded(out_proj, t)
         guarded(relay_sum, t - 1)
-        guarded(forward, t - 3)
-        guarded(share, t - 4)
+        guarded(finish, t - 2, first=final)
+        guarded(share, t - 5, first=final)
+        guarded(collect, t - 6, first=final)
         return carry
-    lax.fori_loop(-1, n_tasks + 5, iteration, 0)
+    lax.fori_loop(-1, n_tasks + 6, iteration, 0)
 
 
 def layers(tp_size, hidden, norm_w, w_z, w_x, w_bc, w_dt, conv_x, conv_bc, bias_x, bias_bc, dt_bias, a_log, d_skip, gate_w, w_out):
@@ -509,7 +518,7 @@
             pltpu.VMEM((state2 // 2, width), F32),
             pltpu.VMEM((3 * state2 // 2, width), BF16),
             pltpu.VMEM((3 * CHUNK, width), BF16),
-            pltpu.VMEM((2, CHUNK, d_model), F32),
+            pltpu.VMEM((P_SLOTS, CHUNK, d_model), F32),
             pltpu.VMEM((2, CHUNK // 2, d_model), F32),
             pltpu.VMEM((SLOTS, 2, piece, d_model), F32),
             pltpu.VMEM((SLOTS, 2, piece, d_model), F32),

time: 158 us -> 157 us (level)
  no operation moved by 1% of the time
where the time goes in v6:
time: 157 us
  Pallas kernels  155 us (99%)
  local copies, waits for them, and re-layouts  1.93 us (1%)
    pallas_call x1, Pallas kernels, layers(): run(hidden[i], norm_w, w_z, w_x, w_bc, w_dt, conv_x, conv_bc, bias_x, bia...  155 us

profile of v6, /device:TPU:81, one launch (start us, length us, event | category | flops | bytes accessed | tf_op | source)
XLA Modules:
  0.0 157.0 jit_solution(12828481801856889243)
XLA Ops:
  0.0 155.0 %shard_map.145 = bf16[768,2560]{1,0:T(8,128)(2,1)S(1)} custom-call(bf16[768,2560]{1,0:T(8,128)(2,1)} %bitcast.4, bf16[2,2560]{1,0:T(2,128)(2,1)} %norm_hbm.1, bf16[2,2560,640]{2,1,0:T(8,128)(2,1)} %wz_hbm.1, bf16[2,2560,640]{2,1,0:T(8,128)(2,1)} %wx_hbm.1, bf16[2,2560,256]{2,1,0:T(8,128)(2,1)} %wbc_hbm.1, bf16[10,2,2560]{2,1,0:T(2,128)(2,1)} %bitcast.5, ...), custom_call_target="tpu_custom_call" | custom-call | tf_op jit(solution)/shard_map/pallas_call | solution.py:536
  155.0 1.9 %copy.17 = bf16[1,768,2560]{2,1,0:T(8,128)(2,1)} copy(bf16[1,768,2560]{2,1,0:T(8,128)(2,1)S(1)} %bitcast.3) | data formatting | bytes 7864320

commit v7 on v6

--- a/solution.py
+++ b/solution.py
@@ -65,7 +65,7 @@
     n_chunks = n_steps // CHUNK
     n_tasks = n_layers * n_chunks
     n_chips = tp_size // 2
-    n_tiles = pre.shape[1] // TILE
+    n_tiles = win.shape[2] // TILE
     half_rows = CHUNK // 2
     slice_rows = half_rows // n_chips
     piece = slice_rows // 2
@@ -213,11 +213,11 @@
 
         @pl.when(row0 == 0)
         def _():
-            pre[0:HALO, :] = jnp.zeros((HALO, pre.shape[1]), F32)
+            pre[:, 0:HALO, :] = jnp.zeros((pre.shape[0], HALO, LANES), F32)
 
         @pl.when(row0 > 0)
         def _():
-            pre[0:HALO, :] = pre[CHUNK:CHUNK + HALO, :]
+            pre[:, 0:HALO, :] = pre[:, CHUNK:CHUNK + HALO, :]
 
         def norm(load):
             def block(i, carry):
@@ -245,9 +245,11 @@
                 wait_in(layer, 2 * i + 1)
             o = pl.multiple_of(i * wide, wide)
             prod = jnp.dot(h[...], win[layer, :, pl.ds(o, wide)], preferred_element_type=F32)
-            pre[HALO:HALO + CHUNK, pl.ds(o, wide)] = prod.astype(BF16).astype(F32)
+            prod = prod.astype(BF16).astype(F32)
+            for j in range(wide // LANES):
+                pre[i * (wide // LANES) + j, HALO:HALO + CHUNK, :] = prod[:, j * LANES:(j + 1) * LANES]
             return carry
-        lax.fori_loop(0, pre.shape[1] // wide, tile, 0)
+        lax.fori_loop(0, n_tiles // 2, tile, 0)
         prod = lax.dot_general(h[...], wdt[layer], (((1,), (1,)), ((), ())), preferred_element_type=F32)
         dtp[:, 0:wdt.shape[1]] = prod.astype(BF16).astype(F32)
 
@@ -280,10 +282,10 @@
             acc = jnp.broadcast_to(cw[layer, conv_width:conv_width + 1, pl.ds(o, LANES)], (CHUNK, LANES))
             for j in range(conv_width):
                 first = HALO - (conv_width - 1) + j
-                acc = acc + pre[first:first + CHUNK, pl.ds(pl.multiple_of(width + o, LANES), LANES)] * cw[layer, j:j + 1, pl.ds(o, LANES)]
+                acc = acc + pre[width // LANES + i, first:first + CHUNK, :] * cw[layer, j:j + 1, pl.ds(o, LANES)]
             act[:, pl.ds(o, LANES)] = silu(acc)
             return carry
-        lax.fori_loop(0, conv_ch // LANES, conv, 0)
+        lax.fori_loop(0, conv_ch // LANES, conv, 0, unroll=True)
 
         row_id = lax.broadcasted_iota(jnp.int32, (CHUNK, CHUNK), 0)
         col_id = lax.broadcasted_iota(jnp.int32, (CHUNK, CHUNK), 1)
@@ -341,7 +343,7 @@
             y = (fast_dot(ml, xh) + fast_dot(mh, xl)) + wide[:, LANES:] + wide[:, :LANES]
             y = y + v[:, cols] * jnp.exp(cum)
             y = y + spread_row(skip) * x
-            gated = y * silu(pre[HALO:HALO + CHUNK, cols])
+            gated = y * silu(pre[p, HALO:HALO + CHUNK, :])
             v[:, cols] = gated
             sq = sq + gated * gated
         total = jnp.sum(sq.T, axis=0, keepdims=True)
@@ -486,6 +488,15 @@
         guarded(collect, t - 6, first=final)
         return carry
     lax.fori_loop(-1, n_tasks + 6, iteration, 0)
+
+
+def write_kernel(src, dst, sem):
+    rows = src.shape[0] // sem.shape[0]
+    copies = [pltpu.make_async_copy(src.at[pl.ds(i * rows, rows)], dst.at[pl.ds(i * rows, rows)], sem.at[i]) for i in range(sem.shape[0])]
+    for cp in copies:
+        cp.start()
+    for cp in copies:
+        cp.wait()
 
 
 def layers(tp_size, hidden, norm_w, w_z, w_x, w_bc, w_dt, conv_x, conv_bc, bias_x, bias_bc, dt_bias, a_log, d_skip, gate_w, w_out):
@@ -510,7 +521,7 @@
             pltpu.VMEM((n_layers, width, d_model), BF16),
             pltpu.VMEM((n_layers, n_steps, d_model), F32),
             pltpu.VMEM((CHUNK, d_model), BF16),
-            pltpu.VMEM((HALO + CHUNK, 2 * width + state2), F32),
+            pltpu.VMEM(((2 * width + state2) // LANES, HALO + CHUNK, LANES), F32),
             pltpu.VMEM((CHUNK, width + state2), F32),
             pltpu.VMEM((CHUNK, width), F32),
             pltpu.VMEM((CHUNK, width), BF16),
@@ -535,7 +546,15 @@
     )
     outs = [run(hidden[i], norm_w, w_z, w_x, w_bc, w_dt, conv_x, conv_bc, bias_x, bias_bc, dt_bias, a_log, d_skip, gate_w, w_out)
             for i in range(n_batch)]
-    return jnp.stack(outs)
+    write = pl.pallas_call(
+        write_kernel,
+        out_shape=jax.ShapeDtypeStruct((n_steps, d_model), BF16),
+        in_specs=[any_spec],
+        out_specs=any_spec,
+        scratch_shapes=[dma((n_steps // CHUNK,))],
+        compiler_params=pltpu.CompilerParams(vmem_limit_bytes=1 << 20),
+    )
+    return jnp.stack([write(out) for out in outs])
 
 
 def solution(mesh):

time: 157 us -> 156 us (level)
  local copies, waits for them, and re-layouts: 1.93 us -> 0 us
    pallas_call x0 -> x1, Pallas kernels: none -> 1.97 us  [layers(): return jnp.stack([write(out) for out in outs])]
    unnamed x1 -> x0, local copies, waits for them, and re-layouts: 1.93 us -> none
where the time goes in v7:
time: 156 us
  Pallas kernels  156 us (100%)
    pallas_call x1, Pallas kernels, layers(): run(hidden[i], norm_w, w_z, w_x, w_bc, w_dt, conv_x, conv_bc, bias_x, bia...  154 us

profile of v7, /device:TPU:81, one launch (start us, length us, event | category | flops | bytes accessed | tf_op | source)
XLA Modules:
  0.0 156.1 jit_solution(12902837406031759612)
XLA Ops:
  0.0 154.1 %shard_map.145.src = bf16[768,2560]{1,0:T(8,128)(2,1)S(1)} custom-call(bf16[768,2560]{1,0:T(8,128)(2,1)} %bitcast.3, bf16[2,2560]{1,0:T(2,128)(2,1)} %norm_hbm.1, bf16[2,2560,640]{2,1,0:T(8,128)(2,1)} %wz_hbm.1, bf16[2,2560,640]{2,1,0:T(8,128)(2,1)} %wx_hbm.1, bf16[2,2560,256]{2,1,0:T(8,128)(2,1)} %wbc_hbm.1, bf16[10,2,2560]{2,1,0:T(2,128)(2,1)} %bitcast.4, ...), custom_call_target="tpu_custom_call" | custom-call | tf_op jit(solution)/shard_map/pallas_call | solution.py:547
  154.1 2.0 %shard_map.146 = bf16[768,2560]{1,0:T(8,128)(2,1)} custom-call(bf16[768,2560]{1,0:T(8,128)(2,1)S(1)} %shard_map.145.src), custom_call_target="tpu_custom_call" | custom-call | tf_op jit(solution)/shard_map/pallas_call | solution.py:557

commit v8 on v7

--- a/solution.py
+++ b/solution.py
@@ -190,13 +190,14 @@
               FW_P: (core, opp, 0), FW_M: (core, opp, 1),
               D0: (1 - core, chip, None), D1: (1 - core, prv, None), D2: (1 - core, nxt, None), D3: (1 - core, opp, None)}
 
-    def msg_ag(t, kind):
+    def msg_ag(t, kind, merged=False):
         j, part, dev = ag_sent[kind]
-        ref = ag_rows(t, core, j, part)
+        ref = ag_rows(t, core, j, None if merged and kind in (OWN_P1, OWN_M1) else part)
         return remote(ref, ref, t, kind, dev)
 
-    def wait_ag(t, kind):
-        ref = ag_rows(t, *ag_got[kind])
+    def wait_ag(t, kind, merged=False):
+        c, j, part = ag_got[kind]
+        ref = ag_rows(t, c, j, None if merged and kind in (OWN_P1, OWN_M1) else part)
         remote(ref, ref, t, kind, dev_sib).wait_recv()
 
     def msg_stat(t, off):
@@ -221,20 +222,20 @@
 
         def norm(load):
             def block(i, carry):
-                r = pl.multiple_of(i * 32, 32)
-                u = load(pl.multiple_of(row0 + r, 32))
+                r = pl.multiple_of(i * 64, 64)
+                u = load(pl.multiple_of(row0 + r, 64))
                 scale = lax.rsqrt(jnp.mean(u * u, axis=-1, keepdims=True) + EPSILON)
-                h[pl.ds(r, 32), :] = (u * scale * nw[layer, 0:1, :]).astype(BF16)
+                h[pl.ds(r, 64), :] = (u * scale * nw[layer, 0:1, :]).astype(BF16)
                 return carry
-            lax.fori_loop(0, CHUNK // 32, block, 0)
+            lax.fori_loop(0, CHUNK // 64, block, 0)
 
         @pl.when(layer == 0)
         def _():
-            norm(lambda r: hid[pl.ds(r, 32), :].astype(F32))
+            norm(lambda r: hid[pl.ds(r, 64), :].astype(F32))
 
         @pl.when(layer > 0)
         def _():
-            norm(lambda r: ures[jnp.maximum(layer - 1, 0), pl.ds(r, 32), :])
+            norm(lambda r: ures[jnp.maximum(layer - 1, 0), pl.ds(r, 64), :])
 
         wide = 2 * TILE
 
@@ -400,7 +401,7 @@
             mine = pl.ds(pl.multiple_of(core * half_rows + r, 8), 8)
             buf[mine, :] = buf[mine, :] + other[pl.ds(r, 8), :]
             return carry
-        lax.fori_loop(0, half_rows // 8, block, 0)
+        lax.fori_loop(0, half_rows // 8, block, 0, unroll=True)
         for kind in (FAR_P, FAR_M, NEAR_P, NEAR_M):
             msg_rs(t, kind).start()
 
@@ -413,7 +414,7 @@
             buf[rows, :] = buf[rows, :] + far[slot, way]
             msg_rs(t, send).start()
 
-    def finish(t):
+    def finish(t, merged):
         slot = lax.rem(t, SLOTS)
         layer, row0 = where_of(t)
         buf = pbuf.at[lax.rem(t, P_SLOTS)]
@@ -434,28 +435,29 @@
         @pl.when(layer > 0)
         def _():
             store(ures[jnp.maximum(layer - 1, 0), dst, :])
-        for kind in (OWN_P1, OWN_M1, OWN_P2, OWN_M2, D0):
-            msg_ag(t, kind).start()
+        for kind in (OWN_P1, OWN_M1, D0) if merged else (OWN_P1, OWN_M1, OWN_P2, OWN_M2, D0):
+            msg_ag(t, kind, merged).start()
         for kind in (SIB, FAR_P, FAR_M, NEAR_P, NEAR_M, COMB_P, COMB_M):
             msg_rs(t, kind).wait_send()
 
-    def forward(t):
+    def forward(t, merged):
         for wait, send in ((OWN_P1, FW_P), (OWN_M1, FW_M)):
-            wait_ag(t, wait)
+            wait_ag(t, wait, merged)
             msg_ag(t, send).start()
 
-    def share(t):
-        for waits, send in (((OWN_P2,), D1), ((OWN_M2,), D2), ((FW_P, FW_M), D3)):
+    def share(t, merged):
+        for waits, send in ((() if merged else (OWN_P2,), D1), (() if merged else (OWN_M2,), D2), ((FW_P, FW_M), D3)):
             for kind in waits:
                 wait_ag(t, kind)
             msg_ag(t, send).start()
 
-    def collect(t):
+    def collect(t, merged):
         layer, row0 = where_of(t)
         for kind in (D0, D1, D2, D3):
             wait_ag(t, kind)
         for kind in ag_sent:
-            msg_ag(t, kind).wait_send()
+            if not (merged and kind in (OWN_P2, OWN_M2)):
+                msg_ag(t, kind, merged).wait_send()
 
         @pl.when(layer == n_layers - 1)
         def _():
@@ -476,27 +478,19 @@
         pl.when(t == -1)(widen)
         guarded(mix, t)
         guarded(pair_sum, t - 1)
-        guarded(forward, t - 4)
-        guarded(share, t - 5, last=final)
-        guarded(collect, t - 5, last=final)
+        guarded(lambda k: forward(k, True), t - 4, last=final)
+        guarded(lambda k: forward(k, False), t - 4, first=final)
+        guarded(lambda k: share(k, True), t - 5, last=final)
+        guarded(lambda k: collect(k, True), t - 5, last=final)
         guarded(in_proj, t + 1)
-        guarded(finish, t - 2, last=final)
+        guarded(lambda k: finish(k, True), t - 2, last=final)
         guarded(out_proj, t)
         guarded(relay_sum, t - 1)
-        guarded(finish, t - 2, first=final)
-        guarded(share, t - 5, first=final)
-        guarded(collect, t - 6, first=final)
+        guarded(lambda k: finish(k, False), t - 2, first=final)
+        guarded(lambda k: share(k, False), t - 5, first=final)
+        guarded(lambda k: collect(k, False), t - 6, first=final)
         return carry
     lax.fori_loop(-1, n_tasks + 6, iteration, 0)
-
-
-def write_kernel(src, dst, sem):
-    rows = src.shape[0] // sem.shape[0]
-    copies = [pltpu.make_async_copy(src.at[pl.ds(i * rows, rows)], dst.at[pl.ds(i * rows, rows)], sem.at[i]) for i in range(sem.shape[0])]
-    for cp in copies:
-        cp.start()
-    for cp in copies:
-        cp.wait()
 
 
 def layers(tp_size, hidden, norm_w, w_z, w_x, w_bc, w_dt, conv_x, conv_bc, bias_x, bias_bc, dt_bias, a_log, d_skip, gate_w, w_out):
@@ -546,15 +540,7 @@
     )
     outs = [run(hidden[i], norm_w, w_z, w_x, w_bc, w_dt, conv_x, conv_bc, bias_x, bias_bc, dt_bias, a_log, d_skip, gate_w, w_out)
             for i in range(n_batch)]
-    write = pl.pallas_call(
-        write_kernel,
-        out_shape=jax.ShapeDtypeStruct((n_steps, d_model), BF16),
-        in_specs=[any_spec],
-        out_specs=any_spec,
-        scratch_shapes=[dma((n_steps // CHUNK,))],
-        compiler_params=pltpu.CompilerParams(vmem_limit_bytes=1 << 20),
-    )
-    return jnp.stack([write(out) for out in outs])
+    return jnp.stack(outs)
 
 
 def solution(mesh):

time: 156 us -> 156 us (level)
  Pallas kernels: 156 us -> 154 us
  local copies, waits for them, and re-layouts: 0 us -> 1.93 us
    pallas_call x1 -> x0, Pallas kernels: 1.97 us -> none  [layers(): return jnp.stack([write(out) for out in outs])]
    unnamed x0 -> x1, local copies, waits for them, and re-layouts: none -> 1.93 us
where the time goes in v8:
time: 156 us
  Pallas kernels  154 us (99%)
  local copies, waits for them, and re-layouts  1.93 us (1%)
    pallas_call x1, Pallas kernels, layers(): run(hidden[i], norm_w, w_z, w_x, w_bc, w_dt, conv_x, conv_bc, bias_x, bia...  154 us

profile of v8, /device:TPU:81, one launch (start us, length us, event | category | flops | bytes accessed | tf_op | source)
XLA Modules:
  0.0 155.7 jit_solution(14820862291827087178)
XLA Ops:
  0.0 153.8 %shard_map.145 = bf16[768,2560]{1,0:T(8,128)(2,1)S(1)} custom-call(bf16[768,2560]{1,0:T(8,128)(2,1)} %bitcast.4, bf16[2,2560]{1,0:T(2,128)(2,1)} %norm_hbm.1, bf16[2,2560,640]{2,1,0:T(8,128)(2,1)} %wz_hbm.1, bf16[2,2560,640]{2,1,0:T(8,128)(2,1)} %wx_hbm.1, bf16[2,2560,256]{2,1,0:T(8,128)(2,1)} %wbc_hbm.1, bf16[10,2,2560]{2,1,0:T(2,128)(2,1)} %bitcast.5, ...), custom_call_target="tpu_custom_call" | custom-call | tf_op jit(solution)/shard_map/pallas_call | solution.py:541
  153.8 1.9 %copy.17 = bf16[1,768,2560]{2,1,0:T(8,128)(2,1)} copy(bf16[1,768,2560]{2,1,0:T(8,128)(2,1)S(1)} %bitcast.3) | data formatting | bytes 7864320
